TPU v7x, 256 devices: a whole 4x4x8 slice. The times are simulated.
256 devices in a mesh: row: 16 (over y, x), col: 16 (over z, core).
Axes of the slice: x: 4, y: 4, z: 8, core: 2. Of those that a mesh axis runs over, the one named last changes fastest.
Arguments:
- matrix: float32 [2, 16, 256, 2, 16, 256], P(None, 'row', None, None, 'col'), as said below
Outputs:
- factored: float32 [2, 16, 256, 2, 16, 256], P(None, 'row', None, None, 'col')
Inputs may be any that keep to these rules, and one draw needn't show every extreme that they name: `matrix`: symmetric and positive definite.
All inputs are finite; a program needn't handle non-finite values.
Results may differ from a plain program's by a relative error of at most 0.0001.
Values sent between devices are 32-bit elements; how exact they have to be, the bound alone decides.
A program may use at most 128 MiB of HBM per device.

v0:
```python
import jax
import jax.numpy as jnp
from jax import lax
from jax.sharding import PartitionSpec as P

STEPS = 8


def broadcast(x, axis, root):
    return lax.dynamic_index_in_dim(lax.all_gather(x, axis), root, 0, keepdims=False)


def solve_panel(factor, column):
    width = column.shape[1]
    inverse = jax.scipy.linalg.solve_triangular(
        factor, jnp.eye(width, dtype=jnp.float32), lower=True
    )
    solved = jnp.einsum("ts,ars->art", inverse, column, precision=lax.Precision.HIGHEST)
    return solved


def on_device(matrix):
    row_tiles = matrix.shape[0]
    width = matrix.shape[2]
    col_tiles = matrix.shape[3]
    tile_grid = matrix.reshape(row_tiles, width, col_tiles, width)
    num_row = lax.axis_size("row")
    num_col = lax.axis_size("col")
    my_row = lax.axis_index("row")
    my_col = lax.axis_index("col")
    rows_global = jnp.arange(row_tiles, dtype=jnp.int32) * num_row + my_row
    ratio = num_col // num_row
    for k in range(STEPS):
        lead_row = k % num_row
        lead_col = k % num_col
        local_row = k // num_row
        local_col = k // num_col
        column = tile_grid[:, :, local_col, :]
        candidate = tile_grid[local_row, :, local_col, :]
        keep = (rows_global > k)[:, None, None]
        diag_tile = broadcast(candidate, "row", lead_row)
        factor = jnp.linalg.cholesky(diag_tile)
        local_panel = jnp.where(keep, solve_panel(factor, column), 0.0)
        panel_rows = broadcast(local_panel, "col", lead_col)
        grouped = panel_rows.reshape(col_tiles, ratio, width, width)
        chosen = lax.dynamic_index_in_dim(grouped, my_col // num_row, 1, keepdims=False)
        panel_cols = broadcast(chosen, "row", my_col % num_row)
        update = jnp.einsum(
            "art,bst->arbs", panel_rows, panel_cols, precision=lax.Precision.HIGHEST
        )
        tile_grid = tile_grid - update
        diagonal_part = jnp.where((rows_global == k)[:, None, None], factor[None], 0.0)
        new_column = panel_rows + diagonal_part
        old_column = tile_grid[:, :, local_col, :]
        tile_grid = tile_grid.at[:, :, local_col, :].set(
            jnp.where(my_col == lead_col, new_column, old_column)
        )
    return tile_grid.reshape(matrix.shape)


def solution(mesh):
    placed = (P(None, "row", None, None, "col", None),)
    return jax.shard_map(
        on_device,
        mesh=mesh,
        in_specs=placed,
        out_specs=P(None, "row", None, None, "col", None),
        check_vma=False,
    )
```

profile of v0, /device:TPU:160, one launch (start us, length us, event | category | flops | bytes accessed | tf_op | source)
XLA Modules:
  0.0 2089.8 jit_solution(10505819206065984409)
XLA Ops:
  8.8 58.6 %all-gather.49.cloned.1.call-done = f32[16,256,1,256]{3,1,2,0:T(8,128)} async-done(((f32[1,256,1,256]{3,1,2,0:T(8,128)}), f32[16,256,1,256]{3,1,2,0:T(8,128)}) %all-gather.49.cloned.1.call-update) | async-done | bytes 4194320 | tf_op jit(solution)/shard_map/all_gather | solution.py:10
  132.1 53.7 %all-gather.51.cloned.1.call-done = f32[32,256,256]{2,1,0:T(8,128)} async-done(((f32[2,256,256]{2,1,0:T(8,128)}), f32[32,256,256]{2,1,0:T(8,128)}) %all-gather.51.cloned.1.call-update) | async-done | bytes 8388624 | tf_op jit(solution)/shard_map/all_gather | solution.py:10
  187.8 76.8 %all-gather.81.cloned.1.call-done = f32[32,256,256]{2,1,0:T(8,128)} async-done(((f32[2,256,256]{2,1,0:T(8,128)}), f32[32,256,256]{2,1,0:T(8,128)}) %all-gather.81.cloned.1.call-update) | async-done | bytes 8388624 | tf_op jit(solution)/shard_map/all_gather | solution.py:10
  269.0 56.3 %all-gather.53.cloned.1.call-done = f32[16,256,1,256]{3,1,2,0:T(8,128)} async-done(((f32[1,256,1,256]{3,1,2,0:T(8,128)}), f32[16,256,1,256]{3,1,2,0:T(8,128)}) %all-gather.53.cloned.1.call-update) | async-done | bytes 4194320 | tf_op jit(solution)/shard_map/all_gather | solution.py:10
  391.1 53.7 %all-gather.55.cloned.1.call-done = f32[32,256,256]{2,1,0:T(8,128)} async-done(((f32[2,256,256]{2,1,0:T(8,128)}), f32[32,256,256]{2,1,0:T(8,128)}) %all-gather.55.cloned.1.call-update) | async-done | bytes 8388624 | tf_op jit(solution)/shard_map/all_gather | solution.py:10
  446.8 76.7 %all-gather.83.cloned.1.call-done = f32[32,256,256]{2,1,0:T(8,128)} async-done(((f32[2,256,256]{2,1,0:T(8,128)}), f32[32,256,256]{2,1,0:T(8,128)}) %all-gather.83.cloned.1.call-update) | async-done | bytes 8388624 | tf_op jit(solution)/shard_map/all_gather | solution.py:10
  527.8 56.3 %all-gather.57.cloned.1.call-done = f32[16,256,1,256]{3,1,2,0:T(8,128)} async-done(((f32[1,256,1,256]{3,1,2,0:T(8,128)}), f32[16,256,1,256]{3,1,2,0:T(8,128)}) %all-gather.57.cloned.1.call-update) | async-done | bytes 4194320 | tf_op jit(solution)/shard_map/all_gather | solution.py:10
  650.1 53.8 %all-gather.59.cloned.1.call-done = f32[32,256,256]{2,1,0:T(8,128)} async-done(((f32[2,256,256]{2,1,0:T(8,128)}), f32[32,256,256]{2,1,0:T(8,128)}) %all-gather.59.cloned.1.call-update) | async-done | bytes 8388624 | tf_op jit(solution)/shard_map/all_gather | solution.py:10
  705.8 76.8 %all-gather.85.cloned.1.call-done = f32[32,256,256]{2,1,0:T(8,128)} async-done(((f32[2,256,256]{2,1,0:T(8,128)}), f32[32,256,256]{2,1,0:T(8,128)}) %all-gather.85.cloned.1.call-update) | async-done | bytes 8388624 | tf_op jit(solution)/shard_map/all_gather | solution.py:10
  787.0 56.3 %all-gather.61.cloned.1.call-done = f32[16,256,1,256]{3,1,2,0:T(8,128)} async-done(((f32[1,256,1,256]{3,1,2,0:T(8,128)}), f32[16,256,1,256]{3,1,2,0:T(8,128)}) %all-gather.61.cloned.1.call-update) | async-done | bytes 4194320 | tf_op jit(solution)/shard_map/all_gather | solution.py:10
  909.1 53.7 %all-gather.63.cloned.1.call-done = f32[32,256,256]{2,1,0:T(8,128)} async-done(((f32[2,256,256]{2,1,0:T(8,128)}), f32[32,256,256]{2,1,0:T(8,128)}) %all-gather.63.cloned.1.call-update) | async-done | bytes 8388624 | tf_op jit(solution)/shard_map/all_gather | solution.py:10
  964.8 76.7 %all-gather.87.cloned.1.call-done = f32[32,256,256]{2,1,0:T(8,128)} async-done(((f32[2,256,256]{2,1,0:T(8,128)}), f32[32,256,256]{2,1,0:T(8,128)}) %all-gather.87.cloned.1.call-update) | async-done | bytes 8388624 | tf_op jit(solution)/shard_map/all_gather | solution.py:10
  1045.9 56.3 %all-gather.65.cloned.1.call-done = f32[16,256,1,256]{3,1,2,0:T(8,128)} async-done(((f32[1,256,1,256]{3,1,2,0:T(8,128)}), f32[16,256,1,256]{3,1,2,0:T(8,128)}) %all-gather.65.cloned.1.call-update) | async-done | bytes 4194320 | tf_op jit(solution)/shard_map/all_gather | solution.py:10
  1168.2 53.7 %all-gather.67.cloned.1.call-done = f32[32,256,256]{2,1,0:T(8,128)} async-done(((f32[2,256,256]{2,1,0:T(8,128)}), f32[32,256,256]{2,1,0:T(8,128)}) %all-gather.67.cloned.1.call-update) | async-done | bytes 8388624 | tf_op jit(solution)/shard_map/all_gather | solution.py:10
  1223.9 76.7 %all-gather.89.cloned.1.call-done = f32[32,256,256]{2,1,0:T(8,128)} async-done(((f32[2,256,256]{2,1,0:T(8,128)}), f32[32,256,256]{2,1,0:T(8,128)}) %all-gather.89.cloned.1.call-update) | async-done | bytes 8388624 | tf_op jit(solution)/shard_map/all_gather | solution.py:10
  1304.9 56.3 %all-gather.69.cloned.1.call-done = f32[16,256,1,256]{3,1,2,0:T(8,128)} async-done(((f32[1,256,1,256]{3,1,2,0:T(8,128)}), f32[16,256,1,256]{3,1,2,0:T(8,128)}) %all-gather.69.cloned.1.call-update) | async-done | bytes 4194320 | tf_op jit(solution)/shard_map/all_gather | solution.py:10
  1427.0 53.7 %all-gather.71.cloned.1.call-done = f32[32,256,256]{2,1,0:T(8,128)} async-done(((f32[2,256,256]{2,1,0:T(8,128)}), f32[32,256,256]{2,1,0:T(8,128)}) %all-gather.71.cloned.1.call-update) | async-done | bytes 8388624 | tf_op jit(solution)/shard_map/all_gather | solution.py:10
  1482.7 76.7 %all-gather.91.cloned.1.call-done = f32[32,256,256]{2,1,0:T(8,128)} async-done(((f32[2,256,256]{2,1,0:T(8,128)}), f32[32,256,256]{2,1,0:T(8,128)}) %all-gather.91.cloned.1.call-update) | async-done | bytes 8388624 | tf_op jit(solution)/shard_map/all_gather | solution.py:10
  1563.7 56.3 %all-gather.73.cloned.1.call-done = f32[16,256,1,256]{3,1,2,0:T(8,128)} async-done(((f32[1,256,1,256]{3,1,2,0:T(8,128)}), f32[16,256,1,256]{3,1,2,0:T(8,128)}) %all-gather.73.cloned.1.call-update) | async-done | bytes 4194320 | tf_op jit(solution)/shard_map/all_gather | solution.py:10
  1686.0 53.7 %all-gather.75.cloned.1.call-done = f32[32,256,256]{2,1,0:T(8,128)} async-done(((f32[2,256,256]{2,1,0:T(8,128)}), f32[32,256,256]{2,1,0:T(8,128)}) %all-gather.75.cloned.1.call-update) | async-done | bytes 8388624 | tf_op jit(solution)/shard_map/all_gather | solution.py:10
  1741.7 76.8 %all-gather.93.cloned.1.call-done = f32[32,256,256]{2,1,0:T(8,128)} async-done(((f32[2,256,256]{2,1,0:T(8,128)}), f32[32,256,256]{2,1,0:T(8,128)}) %all-gather.93.cloned.1.call-update) | async-done | bytes 8388624 | tf_op jit(solution)/shard_map/all_gather | solution.py:10
  1822.9 56.3 %all-gather.77.cloned.1.call-done = f32[16,256,1,256]{3,1,2,0:T(8,128)} async-done(((f32[1,256,1,256]{3,1,2,0:T(8,128)}), f32[16,256,1,256]{3,1,2,0:T(8,128)}) %all-gather.77.cloned.1.call-update) | async-done | bytes 4194320 | tf_op jit(solution)/shard_map/all_gather | solution.py:10
  1944.8 53.7 %all-gather.79.cloned.1.call-done = f32[32,256,256]{2,1,0:T(8,128)} async-done(((f32[2,256,256]{2,1,0:T(8,128)}), f32[32,256,256]{2,1,0:T(8,128)}) %all-gather.79.cloned.1.call-update) | async-done | bytes 8388624 | tf_op jit(solution)/shard_map/all_gather | solution.py:10
  2000.5 76.7 %all-gather.95.cloned.1.call-done = f32[32,256,256]{2,1,0:T(8,128)} async-done(((f32[2,256,256]{2,1,0:T(8,128)}), f32[32,256,256]{2,1,0:T(8,128)}) %all-gather.95.cloned.1.call-update) | async-done | bytes 8388624 | tf_op jit(solution)/shard_map/all_gather | solution.py:10
  (328 shorter events, 599.3 us)
Async XLA Ops:
  6.5 60.8 %all-gather.49.cloned.1.call-start = ((), (), s32[]{:S(2)}) async-start(), calls=%async_computation | async-start | bytes 4456448 | tf_op jit(solution)/shard_map/all_gather | solution.py:10
  8.7 177.2 %all-gather.51.cloned.1.call-start = ((), (), s32[]{:S(2)}) async-start(), calls=%async_computation.1 | async-start | bytes 8912896 | tf_op jit(solution)/shard_map/all_gather | solution.py:10
  132.1 132.6 %all-gather.81.cloned.1.call-start = ((), (), s32[]{:S(2)}) async-start(), calls=%async_computation.16 | async-start | bytes 8912896 | tf_op jit(solution)/shard_map/all_gather | solution.py:10
  187.8 137.5 %all-gather.53.cloned.1.call-start = ((), (), s32[]{:S(2)}) async-start(), calls=%async_computation.2 | async-start | bytes 4456448 | tf_op jit(solution)/shard_map/all_gather | solution.py:10
  269.0 175.9 %all-gather.55.cloned.1.call-start = ((), (), s32[]{:S(2)}) async-start(), calls=%async_computation.3 | async-start | bytes 8912896 | tf_op jit(solution)/shard_map/all_gather | solution.py:10
  391.0 132.4 %all-gather.83.cloned.1.call-start = ((), (), s32[]{:S(2)}) async-start(), calls=%async_computation.17 | async-start | bytes 8912896 | tf_op jit(solution)/shard_map/all_gather | solution.py:10
  446.7 137.4 %all-gather.57.cloned.1.call-start = ((), (), s32[]{:S(2)}) async-start(), calls=%async_computation.4 | async-start | bytes 4456448 | tf_op jit(solution)/shard_map/all_gather | solution.py:10
  527.8 176.1 %all-gather.59.cloned.1.call-start = ((), (), s32[]{:S(2)}) async-start(), calls=%async_computation.5 | async-start | bytes 8912896 | tf_op jit(solution)/shard_map/all_gather | solution.py:10
  650.1 132.6 %all-gather.85.cloned.1.call-start = ((), (), s32[]{:S(2)}) async-start(), calls=%async_computation.18 | async-start | bytes 8912896 | tf_op jit(solution)/shard_map/all_gather | solution.py:10
  705.8 137.5 %all-gather.61.cloned.1.call-start = ((), (), s32[]{:S(2)}) async-start(), calls=%async_computation.6 | async-start | bytes 4456448 | tf_op jit(solution)/shard_map/all_gather | solution.py:10
  787.0 175.9 %all-gather.63.cloned.1.call-start = ((), (), s32[]{:S(2)}) async-start(), calls=%async_computation.7 | async-start | bytes 8912896 | tf_op jit(solution)/shard_map/all_gather | solution.py:10
  909.1 132.4 %all-gather.87.cloned.1.call-start = ((), (), s32[]{:S(2)}) async-start(), calls=%async_computation.19 | async-start | bytes 8912896 | tf_op jit(solution)/shard_map/all_gather | solution.py:10
  964.7 137.4 %all-gather.65.cloned.1.call-start = ((), (), s32[]{:S(2)}) async-start(), calls=%async_computation.8 | async-start | bytes 4456448 | tf_op jit(solution)/shard_map/all_gather | solution.py:10
  1045.8 176.1 %all-gather.67.cloned.1.call-start = ((), (), s32[]{:S(2)}) async-start(), calls=%async_computation.9 | async-start | bytes 8912896 | tf_op jit(solution)/shard_map/all_gather | solution.py:10
  1168.1 132.4 %all-gather.89.cloned.1.call-start = ((), (), s32[]{:S(2)}) async-start(), calls=%async_computation.20 | async-start | bytes 8912896 | tf_op jit(solution)/shard_map/all_gather | solution.py:10
  1223.8 137.4 %all-gather.69.cloned.1.call-start = ((), (), s32[]{:S(2)}) async-start(), calls=%async_computation.10 | async-start | bytes 4456448 | tf_op jit(solution)/shard_map/all_gather | solution.py:10
  1304.8 175.9 %all-gather.71.cloned.1.call-start = ((), (), s32[]{:S(2)}) async-start(), calls=%async_computation.11 | async-start | bytes 8912896 | tf_op jit(solution)/shard_map/all_gather | solution.py:10
  1426.9 132.4 %all-gather.91.cloned.1.call-start = ((), (), s32[]{:S(2)}) async-start(), calls=%async_computation.21 | async-start | bytes 8912896 | tf_op jit(solution)/shard_map/all_gather | solution.py:10
  1482.6 137.4 %all-gather.73.cloned.1.call-start = ((), (), s32[]{:S(2)}) async-start(), calls=%async_computation.12 | async-start | bytes 4456448 | tf_op jit(solution)/shard_map/all_gather | solution.py:10
  1563.7 176.1 %all-gather.75.cloned.1.call-start = ((), (), s32[]{:S(2)}) async-start(), calls=%async_computation.13 | async-start | bytes 8912896 | tf_op jit(solution)/shard_map/all_gather | solution.py:10
  1686.0 132.6 %all-gather.93.cloned.1.call-start = ((), (), s32[]{:S(2)}) async-start(), calls=%async_computation.22 | async-start | bytes 8912896 | tf_op jit(solution)/shard_map/all_gather | solution.py:10
  1741.7 137.5 %all-gather.77.cloned.1.call-start = ((), (), s32[]{:S(2)}) async-start(), calls=%async_computation.14 | async-start | bytes 4456448 | tf_op jit(solution)/shard_map/all_gather | solution.py:10
  1822.9 175.7 %all-gather.79.cloned.1.call-start = ((), (), s32[]{:S(2)}) async-start(), calls=%async_computation.15 | async-start | bytes 8912896 | tf_op jit(solution)/shard_map/all_gather | solution.py:10
  1944.8 132.4 %all-gather.95.cloned.1.call-start = ((), (), s32[]{:S(2)}) async-start(), calls=%async_computation.23 | async-start | bytes 8912896 | tf_op jit(solution)/shard_map/all_gather | solution.py:10
  (1 other events, 258.1 us)
Sparse Core Ops, SparseCore 0:
  9.8 57.5 all-gather.48
  132.2 53.6 all-gather.50
  188.3 76.2 all-gather.80
  269.1 56.1 all-gather.52
  391.2 53.6 all-gather.54
  447.1 76.2 all-gather.82
  527.9 56.1 all-gather.56
  650.2 53.6 all-gather.58
  706.3 76.2 all-gather.84
  787.1 56.1 all-gather.60
  909.2 53.6 all-gather.62
  965.1 76.2 all-gather.86
  1045.9 56.1 all-gather.64
  1168.2 53.6 all-gather.66
  1224.2 76.2 all-gather.88
  1305.0 56.1 all-gather.68
  1427.0 53.6 all-gather.70
  1483.0 76.2 all-gather.90
  1563.8 56.1 all-gather.72
  1686.1 53.6 all-gather.74
  1742.2 76.2 all-gather.92
  1823.0 56.1 all-gather.76
  1944.9 53.6 all-gather.78
  2000.8 76.2 all-gather.94
where the time goes:
time: 2100 us; the launch traced here: 2090 us
  waiting for transfers between devices  1500 us (71%)
  other arithmetic  452 us (22%)
  local copies, waits for them, and re-layouts  65.8 us (3%)
  matrix products  46.6 us (2%)
  between operations  25.1 us (1%)
    all_gather x24, waiting for transfers between devices, broadcast(): lax.all_gather(x, axis)  1500 us
    another operation x55, other arithmetic, on_device(): factor = jnp.linalg.cholesky(diag_tile)  276 us
    another operation x17, other arithmetic, solve_panel(): jax.scipy.linalg.solve_triangular(factor, jnp.eye(width, dtype=jnp.float3...  158 us
  transfers between devices with their start and end apart: 24, of which 24 were waited for; matrix products, arithmetic and copies ran while one was open for 0% of the time, Pallas kernels for 0%

commit v1 on v0

v1 whole, which is shorter than its diff:
```python
import jax, jax.numpy as jnp, functools
from jax import lax
from jax.experimental import pallas as pl
from jax.experimental.pallas import tpu as pltpu

F32, BF16 = jnp.float32, jnp.bfloat16

def over_lanes(v, c):
    return jnp.broadcast_to(v[:, c:c + 1], (8, 128))

def over_rows(v, r):
    return jnp.broadcast_to(v[r:r + 1, :], (8, 128))

def eliminate(rows):
    sub = lax.broadcasted_iota(jnp.int32, (8, 128), 0)
    rows = list(rows)
    diag = [over_lanes(rows[0], t) for t in range(8)]
    for s in range(8):
        off = {i: [over_lanes(rows[i], 8 * s + m) for m in range(8)] for i in range(s + 1, 8)}
        nxt = [over_lanes(rows[s + 1], 8 * (s + 1) + t) for t in range(8)] if s < 7 else None
        top = rows[s]
        for m in range(8):
            root = lax.rsqrt(over_rows(diag[m], m))
            lead = diag[m] * root
            unit = over_rows(top, m) * root
            top = jnp.where(sub == m, unit, top - jnp.where(sub > m, lead, 0.0) * unit)
            scal = {t: over_rows(lead, t) for t in range(m + 1, 8)}
            for t in range(m + 1, 8):
                diag[t] = diag[t] - lead * scal[t]
            for i in range(s + 1, 8):
                mult = off[i][m] * root
                for t in range(m + 1, 8):
                    off[i][t] = off[i][t] - mult * scal[t]
                rows[i] = rows[i] - mult * unit
                if i == s + 1:
                    for t in range(8):
                        nxt[t] = nxt[t] - mult * over_rows(mult, t)
        rows[s] = top
        diag = nxt
    return rows

def split(x):
    hi = x.astype(BF16)
    return hi, (x - hi.astype(F32)).astype(BF16)

def nt(a, b):
    return lax.dot_general(a, b, (((1,), (1,)), ((), ())), preferred_element_type=F32)

def nn(a, b):
    return lax.dot_general(a, b, (((1,), (0,)), ((), ())), preferred_element_type=F32)

def factor_tile(tb, ud, lb, zpad, w_hi, w_lo):
    low = lax.broadcasted_iota(jnp.int32, (64, 128), 1) < 64
    eye = jnp.where(
        lax.broadcasted_iota(jnp.int32, (64, 128), 1)
        == lax.broadcasted_iota(jnp.int32, (64, 128), 0) + 64, 1.0, 0.0).astype(F32)
    zpad[...] = jnp.zeros_like(zpad)

    def group(g, _):
        block = jnp.where(low, tb[g, g], eye)
        done = eliminate([block[8 * i:8 * i + 8] for i in range(8)])
        m = jnp.concatenate(done, 0)
        ud[g] = m
        wz = jnp.where(low, 0.0, m)
        wz_hi, wz_lo = split(wz)
        tcol = tb[:, g].reshape(256, 128)
        t_hi, t_lo = split(tcol)
        w2_hi = jnp.concatenate([wz_hi, wz_hi], 0)
        w2_lo = jnp.concatenate([wz_lo, wz_lo], 0)
        p = nt(jnp.concatenate([t_hi, t_lo], 1), jnp.concatenate([w2_hi, w2_hi], 1)) + nt(t_hi, w2_lo)
        rowblk = lax.broadcasted_iota(jnp.int32, (256, 128), 0) // 64
        p = jnp.where(rowblk > g, p, 0.0)
        lb[:, g] = p.reshape(4, 64, 128)
        hi = p.astype(BF16)
        hif = hi.astype(F32)
        lof = p - hif
        lo = lof.astype(BF16)
        lowp = lax.broadcasted_iota(jnp.int32, (256, 128), 1) < 64
        lhs = jnp.concatenate([jnp.where(lowp, hif, lof).astype(BF16),
                               jnp.where(lowp, hif, 0.0).astype(BF16)], 1)
        for h in range(2):
            parts = []
            for j in (2 * h, 2 * h + 1):
                pj = jnp.concatenate([hi[64 * j:64 * j + 64], lo[64 * j:64 * j + 64]], 1)
                parts += [pj, pj]
            upd = nt(lhs, jnp.concatenate(parts, 0))
            for j in range(2):
                tb[:, 2 * h + j] = tb[:, 2 * h + j] - upd[:, 128 * j:128 * j + 128].reshape(4, 64, 128)
        z = zpad[pl.ds(pl.multiple_of(64 * g, 64), 128), :]
        z_hi, z_lo = split(z)
        mix = nn(jnp.concatenate([wz_hi, wz_lo], 1), jnp.concatenate([z_hi, z_hi], 0)) + nn(wz_hi, z_lo)
        turned = pltpu.roll(m, 64, 1)
        both = jnp.where(low, turned, m)
        here = lax.broadcasted_iota(jnp.int32, (64, 256), 1) // 64 == g
        wrow = jnp.where(here, jnp.concatenate([both, both], 1), -mix)
        at = pl.ds(pl.multiple_of(64 * g, 64), 64)
        r_hi, r_lo = split(wrow)
        w_hi[at, :] = r_hi
        w_lo[at, :] = r_lo
        zpad[64:, :] = zpad[64:, :] + nn(lhs, jnp.concatenate([r_hi, r_hi, r_lo, r_lo], 0))
        return 0
    lax.fori_loop(0, 4, group, 0)

def blocks(tile, tb):
    low = lax.broadcasted_iota(jnp.int32, (256, 128), 1) < 64
    for h in range(2):
        x = tile[:, 128 * h:128 * h + 128]
        r = pltpu.roll(x, 64, 1)
        tb[:, 2 * h] = jnp.where(low, x, r).reshape(4, 64, 128)
        tb[:, 2 * h + 1] = jnp.where(low, r, x).reshape(4, 64, 128)


B = 256
STEPS = 8
SLOTS = 10

def nt3(ah, al, bh, bl):
    return nt(ah, bh) + nt(ah, bl) + nt(al, bh)

def nn3(ah, al, bh, bl):
    return nn(ah, bh) + nn(ah, bl) + nn(al, bh)

def local_kernel(p, q, d_ref, x_ref, y_ref, own_ref, out_ref,
                 g, lh, ll, uh, ul, y, tb, ud, lb, zpad, wh, wl, held, g_sem, y_sem):
    copies = []
    for k in range(STEPS):
        mine = [pltpu.make_async_copy(d_ref.at[k, i], g.at[k, i], g_sem.at[k, i]) for i in range(k, STEPS)]
        mine += [pltpu.make_async_copy(x_ref.at[k, a], g.at[k, STEPS + a], g_sem.at[k, STEPS + a]) for a in range(2)]
        mine += [pltpu.make_async_copy(y_ref.at[k], y.at[k], y_sem.at[k])]
        copies.append(mine)
        for c in mine:
            c.start()
    out_ref[...] = own_ref[...]

    def step(k, _):
        def arrive(i, _):
            pltpu.make_async_copy(d_ref.at[k, i], g.at[k, i], g_sem.at[k, i]).wait()
            return 0
        lax.fori_loop(k, STEPS, arrive, 0)
        for a in range(2):
            pltpu.make_async_copy(x_ref.at[k, a], g.at[k, STEPS + a], g_sem.at[k, STEPS + a]).wait()
        pltpu.make_async_copy(y_ref.at[k], y.at[k], y_sem.at[k]).wait()

        def pair(r):
            return pl.ds(2 * r, 2)

        def update(r, _):
            def term(m, _):
                got = nt3(lh[m, pair(r)].reshape(512, B), ll[m, pair(r)].reshape(512, B), lh[m, k], ll[m, k])
                g[k, pair(r)] = g[k, pair(r)] - got.reshape(2, B, B)
                return 0
            return lax.fori_loop(0, k, term, 0)
        lax.fori_loop(k // 2, 5, update, 0)

        blocks(g[k, k], tb)
        factor_tile(tb, ud, lb, zpad, wh, wl)

        def solve(r, _):
            ah, al = split(g[k, pair(r)].reshape(512, B))
            got = nt3(ah, al, wh[...], wl[...]).reshape(2, B, B)
            hi, lo = split(got)
            lh[k, pair(r)] = hi
            ll[k, pair(r)] = lo
            return 0
        lax.fori_loop(k // 2, 4, solve, 0)

        ah, al = split(g[k, 8:10].reshape(512, B))
        got = nt3(ah, al, wh[...], wl[...])
        got = jnp.concatenate([jnp.where(p > k, got[:B], 0.0), got[B:]], 0)
        hi, lo = split(got)
        lh[k, 8:10] = hi.reshape(2, B, B)
        ll[k, 8:10] = lo.reshape(2, B, B)

        @pl.when(q == k)
        def _():
            held[...] = got.reshape(2, B, B)

        @pl.when((q == k) & (p == k))
        def _():
            low = lax.broadcasted_iota(jnp.int32, (64, 128), 1) < 64
            tri = lax.broadcasted_iota(jnp.int32, (64, 128), 0) <= lax.broadcasted_iota(jnp.int32, (64, 128), 1)
            for i in range(4):
                up = jnp.where(tri & low, ud[i], 0.0)
                turned = jnp.concatenate([up, jnp.zeros((64, 128), F32)], 0).T[:64]
                twice = turned + pltpu.roll(turned, 64, 1)
                parts = [lb[i, j] if j < i else (twice if j == i else jnp.zeros((64, 128), F32)) for j in range(4)]
                for h in range(2):
                    held[0, 64 * i:64 * i + 64, 128 * h:128 * h + 128] = jnp.where(low, parts[2 * h], parts[2 * h + 1])

        def uterm(m, _):
            y[k] = y[k] - nn3(lh[m, k], ll[m, k], uh[m], ul[m])
            return 0
        lax.fori_loop(0, k, uterm, 0)
        yh, yl = split(y[k])
        u = nn3(wh[...], wl[...], yh, yl)
        u = jnp.concatenate([jnp.where(q > k, u[:, :B], 0.0), u[:, B:]], 1)
        hi, lo = split(u)
        uh[k] = hi
        ul[k] = lo
        for a in range(2):
            out_ref[a] = out_ref[a] - nn3(lh[k, 8 + a], ll[k, 8 + a], hi, lo)
        return 0
    lax.fori_loop(0, STEPS, step, 0)

    @pl.when(q < STEPS)
    def _():
        out_ref[:, :, :B] = held[...]

def scratch():
    V = pltpu.VMEM
    return [V((STEPS, SLOTS, B, B), F32), V((STEPS, SLOTS, B, B), BF16), V((STEPS, SLOTS, B, B), BF16),
            V((STEPS, B, 2 * B), BF16), V((STEPS, B, 2 * B), BF16), V((STEPS, B, 2 * B), F32),
            V((4, 4, 64, 128), F32), V((4, 64, 128), F32), V((4, 4, 64, 128), F32), V((320, B), F32),
            V((B, B), BF16), V((B, B), BF16), V((2, B, B), F32),
            pltpu.SemaphoreType.DMA((STEPS, SLOTS)), pltpu.SemaphoreType.DMA((STEPS,))]

from jax.sharding import PartitionSpec as P


def local_entry(*refs):
    local_kernel(lax.axis_index("row"), lax.axis_index("col"), *refs)


def on_device(matrix):
    own = matrix.reshape(2, B, 2 * B)
    x = lax.all_gather(own[:, :, :B], "col")
    y = lax.all_gather(own[0], "row")
    d = lax.all_gather(y[:STEPS, :, :B], "col")
    out = pl.pallas_call(
        local_entry,
        out_shape=jax.ShapeDtypeStruct((2, B, 2 * B), F32),
        in_specs=[pl.BlockSpec(memory_space=pl.ANY)] * 3 + [pl.BlockSpec(memory_space=pltpu.VMEM)],
        out_specs=pl.BlockSpec(memory_space=pltpu.VMEM),
        scratch_shapes=scratch(),
        compiler_params=pltpu.CompilerParams(vmem_limit_bytes=63 * 1024 * 1024),
    )(d, x, y, own)
    return out.reshape(matrix.shape)


def solution(mesh):
    spec = P(None, "row", None, None, "col", None)
    return jax.shard_map(on_device, mesh=mesh, in_specs=(spec,), out_specs=spec, check_vma=False)
```

time: 2100 us -> 459 us (0.22)
  waiting for transfers between devices: 1500 us -> 297 us
  other arithmetic: 452 us -> 4.28 us
  Pallas kernels: 0 us -> 126 us
  local copies, waits for them, and re-layouts: 65.8 us -> 13.1 us
  matrix products: 46.6 us -> 0 us
    all_gather x24 -> x3, waiting for transfers between devices: 1500 us -> 297 us  [the longest x1 175 us: on_device(): d = lax.all_gather(y[:STEPS, :, :B], 'col')]
    another operation x72 -> x0, other arithmetic: 434 us -> none  [the longest x55 276 us: on_device(): factor = jnp.linalg.cholesky(diag_tile)]
    pallas_call x0 -> x1, Pallas kernels: none -> 126 us  [on_device(): pl.pallas_call(local_entry, out_shape=jax.ShapeDtypeStruct((2, B, 2 * B),...]
    dot_general x16 -> x0, matrix products: 35.8 us -> none  [the longest x8 18 us: solve_panel(): jnp.einsum('ts,ars->art', inverse, column, precision=lax.Precision.HIGHEST)]
    another operation x73 -> x0, local copies, waits for them, and re-layouts: 31.3 us -> none  [the longest x57 31.1 us: solve_panel(): jax.scipy.linalg.solve_triangular(factor, jnp.eye(width, dtype=jnp.float3...]
    dynamic_slice x16 -> x0, local copies, waits for them, and re-layouts: 22.7 us -> none  [broadcast(): lax.dynamic_index_in_dim(lax.all_gather(x, axis), root, 0, keepdims=False)]
  transfers between devices with their start and end apart: 24 -> 3, of which waited for: 24 -> 3; matrix products, arithmetic and copies ran while one was open for 0% -> 2% of each run, Pallas kernels for 0% -> 0%
where the time goes in v1:
time: 459 us; the launch traced here: 454 us
  waiting for transfers between devices  297 us (65%)
  Pallas kernels  126 us (27%)
  local copies, waits for them, and re-layouts  13.1 us (3%)
  between operations  13.1 us (3%)
    all_gather x1, waiting for transfers between devices, on_device(): d = lax.all_gather(y[:STEPS, :, :B], 'col')  175 us
    pallas_call x1, Pallas kernels, on_device(): pl.pallas_call(local_entry, out_shape=jax.ShapeDtypeStruct((2, B, 2 * B),...  126 us
    all_gather x1, waiting for transfers between devices, on_device(): y = lax.all_gather(own[0], 'row')  70 us
    all_gather x1, waiting for transfers between devices, on_device(): x = lax.all_gather(own[:, :, :B], 'col')  52.4 us
  transfers between devices with their start and end apart: 3, of which 3 were waited for; matrix products, arithmetic and copies ran while one was open for 2% of the time, Pallas kernels for 0%

profile of v1, /device:TPU:160, one launch (start us, length us, event | category | flops | bytes accessed | tf_op | source)
XLA Modules:
  0.0 453.5 jit_solution(6294263383247597191)
XLA Ops:
  6.5 0.0 all-gather.6.cloned.1.call-start
  6.5 2.7 slice_reduce_fusion
  9.2 1.2 slice.13
  10.5 0.0 all-gather.6.cloned.1.call-update
  10.5 0.0 all-gather.10.cloned.1.call-start
  10.5 4.3 reduce.1
  14.8 0.8 reshape.7.refs_3_
  15.7 0.0 copy-start
  15.7 1.0 copy-done
  16.6 0.8 slice.17
  17.5 0.0 all-gather.10.cloned.1.call-update
  17.5 0.0 all-gather.8.cloned.1.call-start
  17.6 70.0 %all-gather.6.cloned.1.call-done.refs_2_ = f32[16,256,512]{2,1,0:T(8,128)} async-done(((f32[1,256,512]{2,1,0:T(8,128)}), f32[16,256,512]{2,1,0:T(8,128)}) %all-gather.6.cloned.1.call-update) | async-done | bytes 8388624 | tf_op jit(solution)/shard_map/all_gather | solution.py:227
  87.6 3.1 slice.16
  90.7 0.0 all-gather.8.cloned.1.call-update
  90.7 52.4 %all-gather.10.cloned.1.call-done = f32[32,256,256]{2,1,0:T(8,128)} async-done(((f32[2,256,256]{2,1,0:T(8,128)}), f32[32,256,256]{2,1,0:T(8,128)}) %all-gather.10.cloned.1.call-update) | async-done | bytes 8388624 | tf_op jit(solution)/shard_map/all_gather | solution.py:226
  143.1 174.8 %all-gather.8.cloned.1.call-done = f32[128,256,256]{2,1,0:T(8,128)} async-done(((f32[8,256,256]{2,1,0:T(8,128)}), f32[128,256,256]{2,1,0:T(8,128)}) %all-gather.8.cloned.1.call-update) | async-done | bytes 33554448 | tf_op jit(solution)/shard_map/all_gather | solution.py:228
  317.9 125.7 %shard_map.17 = f32[2,256,512]{2,1,0:T(8,128)} custom-call(f32[16,8,256,256]{3,2,1,0:T(8,128)} %bitcast.2, f32[16,2,256,256]{3,2,1,0:T(8,128)} %bitcast.3, f32[16,256,512]{2,1,0:T(8,128)} %all-gather.6.cloned.1.call-done.refs_2_, f32[2,256,512]{2,1,0:T(8,128)} %copy-done), custom_call_target="tpu_custom_call" | custom-call | tf_op jit(solution)/shard_map/pallas_call | solution.py:229
  443.6 3.4 reshape.11
Async XLA Ops:
  6.5 81.1 %all-gather.6.cloned.1.call-start = ((), (), s32[]{:S(2)}) async-start(), calls=%async_computation | async-start | bytes 8912896 | tf_op jit(solution)/shard_map/all_gather | solution.py:227
  10.5 132.6 %all-gather.10.cloned.1.call-start = ((), (), s32[]{:S(2)}) async-start(), calls=%async_computation.2 | async-start | bytes 8912896 | tf_op jit(solution)/shard_map/all_gather | solution.py:226
  15.7 1.0 copy-start
  17.5 300.4 %all-gather.8.cloned.1.call-start = ((), (), s32[]{:S(2)}) async-start(), calls=%async_computation.1 | async-start | bytes 35651584 | tf_op jit(solution)/shard_map/all_gather | solution.py:228
Sparse Core Ops, SparseCore 0:
  10.6 76.9 all-gather.5
  89.4 53.6 all-gather.9
  144.9 172.9 all-gather.7

commit v2 on v1

--- a/solution.py
+++ b/solution.py
@@ -120,26 +120,23 @@
 def nn3(ah, al, bh, bl):
     return nn(ah, bh) + nn(ah, bl) + nn(al, bh)
 
-def local_kernel(p, q, d_ref, x_ref, y_ref, own_ref, out_ref,
+def local_kernel(p, q, g_in, y_in, own_ref, out_ref,
                  g, lh, ll, uh, ul, y, tb, ud, lb, zpad, wh, wl, held, g_sem, y_sem):
-    copies = []
+    def slot_of(i):
+        return jnp.where((i == p) & (i < STEPS), STEPS, i)
+
     for k in range(STEPS):
-        mine = [pltpu.make_async_copy(d_ref.at[k, i], g.at[k, i], g_sem.at[k, i]) for i in range(k, STEPS)]
-        mine += [pltpu.make_async_copy(x_ref.at[k, a], g.at[k, STEPS + a], g_sem.at[k, STEPS + a]) for a in range(2)]
-        mine += [pltpu.make_async_copy(y_ref.at[k], y.at[k], y_sem.at[k])]
-        copies.append(mine)
-        for c in mine:
-            c.start()
+        for i in range(k, SLOTS):
+            pltpu.make_async_copy(g_in.at[k, slot_of(i)], g.at[k, i], g_sem.at[k, i]).start()
+        pltpu.make_async_copy(y_in.at[k], y.at[k], y_sem.at[k]).start()
     out_ref[...] = own_ref[...]
 
     def step(k, _):
         def arrive(i, _):
-            pltpu.make_async_copy(d_ref.at[k, i], g.at[k, i], g_sem.at[k, i]).wait()
+            pltpu.make_async_copy(g_in.at[k, i], g.at[k, i], g_sem.at[k, i]).wait()
             return 0
-        lax.fori_loop(k, STEPS, arrive, 0)
-        for a in range(2):
-            pltpu.make_async_copy(x_ref.at[k, a], g.at[k, STEPS + a], g_sem.at[k, STEPS + a]).wait()
-        pltpu.make_async_copy(y_ref.at[k], y.at[k], y_sem.at[k]).wait()
+        lax.fori_loop(k, SLOTS, arrive, 0)
+        pltpu.make_async_copy(y_in.at[k], y.at[k], y_sem.at[k]).wait()
 
         def pair(r):
             return pl.ds(2 * r, 2)
@@ -213,27 +210,234 @@
             V((4, 4, 64, 128), F32), V((4, 64, 128), F32), V((4, 4, 64, 128), F32), V((320, B), F32),
             V((B, B), BF16), V((B, B), BF16), V((2, B, B), F32),
             pltpu.SemaphoreType.DMA((STEPS, SLOTS)), pltpu.SemaphoreType.DMA((STEPS,))]
+MESH = pl.DeviceIdType.MESH
+
+class Comm:
+    def __init__(self, p, q, own, g, y, send_sem, g_sem, y_sem, x_sem, d_sem, own_sem):
+        self.p, self.q, self.own, self.g, self.y = p, q, own, g, y
+        self.px, self.py, self.pz, self.c = p % 4, p // 4, q // 2, q % 2
+        self.send_sem, self.g_sem, self.y_sem = send_sem, g_sem, y_sem
+        self.x_sem, self.d_sem, self.own_sem = x_sem, d_sem, own_sem
+        self.sent = []
+
+    def at_z(self, d):
+        return (self.p, 2 * ((self.pz + d) % 8) + self.c)
+
+    def at_y(self, d):
+        return (4 * ((self.py + d) % 4) + self.px, self.q)
+
+    def at_x(self, d):
+        return (4 * self.py + (self.px + d) % 4, self.q)
+
+    def sibling(self):
+        return (self.p, 2 * self.pz + 1 - self.c)
+
+    def barrier(self):
+        b = pltpu.get_barrier_semaphore()
+        peers = [self.at_z(1), self.at_z(-1), self.at_y(1), self.at_y(-1), self.at_x(1), self.at_x(-1), self.sibling()]
+        for d in peers:
+            pl.semaphore_signal(b, inc=1, device_id=d, device_id_type=MESH)
+        pl.semaphore_wait(b, len(peers))
+
+    def send(self, cond, src, dst, sem, to):
+        c = pltpu.make_async_remote_copy(src_ref=src, dst_ref=dst, send_sem=self.send_sem.at[len(self.sent)],
+                                         recv_sem=sem, device_id=to, device_id_type=MESH)
+        pl.when(cond)(c.start)
+        self.sent.append((cond, c))
+
+    def take(self, cond, ref, sem):
+        c = pltpu.make_async_remote_copy(src_ref=ref, dst_ref=ref, send_sem=self.send_sem.at[0],
+                                         recv_sem=sem, device_id=self.sibling(), device_id_type=MESH)
+        pl.when(cond)(c.wait_recv)
+
+    def drain(self):
+        for cond, c in self.sent:
+            pl.when(cond)(c.wait_send)
+
+    def local(self):
+        p, q = self.p, self.q
+        lead = jnp.minimum(q, 7)
+        rowk = jnp.minimum(p, 7)
+        return [(q < 8, pltpu.make_async_copy(self.own.at[a, :, pl.ds(0, B)], self.g.at[lead, 8 + a], self.own_sem.at[a]))
+                for a in range(2)] + [
+            (p < 8, pltpu.make_async_copy(self.own.at[0], self.y.at[rowk], self.own_sem.at[2]))]
+
+    def gp(self, k, slot, piece):
+        return self.g.at[k, slot, pl.ds(64 * piece, 64)]
+
+    def z_hop(self, s):
+        for d, pieces in ((1, (0, 1)), (-1, (2, 3))):
+            zs = (self.pz - d * s) % 8
+            on = zs < 4
+            k = jnp.minimum(2 * zs + self.c, 7)
+            for a in range(2):
+                for piece in pieces:
+                    ref, sem = self.gp(k, 8 + a, piece), self.g_sem.at[k, 8 + a, piece]
+                    if s > 0:
+                        self.take(on, ref, sem)
+                    if s < 7:
+                        self.send(on, ref, ref, sem, self.at_z(d))
+                    if a == 0:
+                        row = on & (self.p < 8) & (k <= self.p)
+                        pp = jnp.minimum(self.p, 7)
+                        for e in (1, -1):
+                            self.send(row, ref, self.gp(k, pp, piece), self.g_sem.at[k, pp, piece], self.at_y(e))
+
+    def y_own(self):
+        pp = jnp.minimum(self.p, 7)
+        for piece in range(4):
+            ref = self.y.at[pp, pl.ds(64 * piece, 64)]
+            for e in (1, -1):
+                self.send(self.p < 8, ref, ref, self.y_sem.at[pp, piece], self.at_y(e))
+
+    def item(self, k):
+        if k is None:
+            ref = lambda r, piece: self.y.at[r, pl.ds(64 * piece, 64)]
+            return ref, ref, (lambda r, piece: self.y_sem.at[r, piece]), (lambda r: True)
+        return ((lambda r, piece: self.gp(k, jnp.where(r == self.p, 8, r), piece)),
+                (lambda r, piece: self.gp(k, r, piece)),
+                (lambda r, piece: self.g_sem.at[k, r, piece]),
+                (lambda r: k <= r))
+
+    def y_forward(self, k):
+        src, dst, sem, has = self.item(k)
+        for d, pieces in ((1, (0, 1)), (-1, (2, 3))):
+            ys = (self.py - d) % 4
+            r = jnp.minimum(4 * ys + self.px, 7)
+            on = (ys < 2) & has(r)
+            for piece in pieces:
+                self.take(on, dst(r, piece), sem(r, piece))
+                self.send(on, dst(r, piece), dst(r, piece), sem(r, piece), self.at_y(d))
+
+    def x_send(self, k):
+        src, dst, sem, has = self.item(k)
+        for ys in range(2):
+            r = 4 * ys + self.px
+            dist = (self.py - ys) % 4
+            for piece in range(4):
+                rest = (dist == 2) | (dist == (1 if piece >= 2 else 3))
+                self.take(rest & has(r), dst(r, piece), sem(r, piece))
+                for e in (1, -1):
+                    self.send(jnp.bool_(True) & has(r), src(r, piece), dst(r, piece), sem(r, piece), self.at_x(e))
+            if k is not None:
+                self.send(has(r) & (dist != 0), self.g.at[k, r], self.g.at[k, r], self.d_sem.at[k, r], self.sibling())
+
+    def x_forward(self, k):
+        src, dst, sem, has = self.item(k)
+        for d, pieces in ((1, (0, 1)), (-1, (2, 3))):
+            xs = (self.px - d) % 4
+            for ys in range(2):
+                r = 4 * ys + xs
+                for piece in pieces:
+                    self.take(jnp.bool_(True) & has(r), dst(r, piece), sem(r, piece))
+                    self.send(jnp.bool_(True) & has(r), dst(r, piece), dst(r, piece), sem(r, piece), self.at_x(d))
+
+    def finish(self, k):
+        src, dst, sem, has = self.item(k)
+        for dx in (1, 3, 2):
+            xs = (self.px - dx) % 4
+            pieces = {1: (2, 3), 3: (0, 1), 2: (0, 1, 2, 3)}[dx]
+            for ys in range(2):
+                r = 4 * ys + xs
+                for piece in pieces:
+                    self.take(jnp.bool_(True) & has(r), dst(r, piece), sem(r, piece))
+                if k is not None:
+                    self.send(has(r), self.g.at[k, r], self.g.at[k, r], self.d_sem.at[k, r], self.sibling())
+
+    def x_sibling(self):
+        for i in range(4):
+            k = 2 * i + self.c
+            self.send(jnp.bool_(True) & (k < 8), self.g.at[k, pl.ds(8, 2)], self.g.at[k, pl.ds(8, 2)], self.x_sem.at[k], self.sibling())
+
+    def from_sibling(self):
+        for i in range(4):
+            k = 2 * i + 1 - self.c
+            self.take(k < 8, self.g.at[k, pl.ds(8, 2)], self.x_sem.at[k])
+            for r in range(8):
+                self.take((k <= r) & (r != self.p), self.g.at[k, r], self.d_sem.at[k, r])
+
+    def run(self):
+        mine = self.local()
+        for on, c in mine:
+            pl.when(on)(c.start)
+        self.barrier()
+        for on, c in mine:
+            pl.when(on)(c.wait)
+        ks = [2 * i + self.c for i in range(4)]
+        self.z_hop(0)
+        self.y_own()
+        self.z_hop(1)
+        self.z_hop(2)
+        self.y_forward(None)
+        self.z_hop(3)
+        self.x_send(None)
+        self.z_hop(4)
+        self.x_forward(None)
+        self.z_hop(5)
+        self.z_hop(6)
+        self.z_hop(7)
+        self.x_sibling()
+        for k in ks:
+            self.y_forward(k)
+        for k in ks:
+            self.x_send(k)
+        for k in ks:
+            self.x_forward(k)
+        for k in ks:
+            self.finish(k)
+        self.finish(None)
+        self.from_sibling()
+        self.drain()
+
+N_SEND = 640
+
+def comm_scratch():
+    D = pltpu.SemaphoreType.DMA
+    return [D((N_SEND,)), D((8, 10, 4)), D((8, 4)), D((8,)), D((8, 8)), D((3,))]
 
 from jax.sharding import PartitionSpec as P
 
 
-def local_entry(*refs):
-    local_kernel(lax.axis_index("row"), lax.axis_index("col"), *refs)
+def gather_entry(own, g_out, y_out, g, y, out_sem, *sems):
+    p, q = lax.axis_index("row"), lax.axis_index("col")
+    Comm(p, q, own, g, y, *sems).run()
+    outs = [pltpu.make_async_copy(y, y_out, out_sem.at[0])]
+    for k in range(8):
+        outs.append(pltpu.make_async_copy(g.at[k, pl.ds(k, 10 - k)], g_out.at[k, pl.ds(k, 10 - k)], out_sem.at[1 + k]))
+
+    row = jnp.minimum(p, 7)
+    for c in outs:
+        c.start()
+    for c in outs:
+        c.wait()
+
+
+def local_entry(g_in, y_in, own_ref, out_ref, *rest):
+    local_kernel(lax.axis_index("row"), lax.axis_index("col"), g_in, y_in, own_ref, out_ref, *rest)
 
 
 def on_device(matrix):
     own = matrix.reshape(2, B, 2 * B)
-    x = lax.all_gather(own[:, :, :B], "col")
-    y = lax.all_gather(own[0], "row")
-    d = lax.all_gather(y[:STEPS, :, :B], "col")
+    any_spec = pl.BlockSpec(memory_space=pl.ANY)
+    g, y = pl.pallas_call(
+        gather_entry,
+        out_shape=[jax.ShapeDtypeStruct((STEPS, SLOTS, B, B), F32), jax.ShapeDtypeStruct((STEPS, B, 2 * B), F32)],
+        in_specs=[any_spec],
+        out_specs=[any_spec] * 2,
+        scratch_shapes=[pltpu.VMEM((STEPS, SLOTS, B, B), F32), pltpu.VMEM((STEPS, B, 2 * B), F32),
+                        pltpu.SemaphoreType.DMA((9,))] + comm_scratch(),
+        compiler_params=pltpu.CompilerParams(vmem_limit_bytes=63 * 1024 * 1024, collective_id=0, has_side_effects=True),
+        name="gather",
+    )(own)
     out = pl.pallas_call(
         local_entry,
         out_shape=jax.ShapeDtypeStruct((2, B, 2 * B), F32),
-        in_specs=[pl.BlockSpec(memory_space=pl.ANY)] * 3 + [pl.BlockSpec(memory_space=pltpu.VMEM)],
+        in_specs=[any_spec] * 2 + [pl.BlockSpec(memory_space=pltpu.VMEM)],
         out_specs=pl.BlockSpec(memory_space=pltpu.VMEM),
         scratch_shapes=scratch(),
         compiler_params=pltpu.CompilerParams(vmem_limit_bytes=63 * 1024 * 1024),
-    )(d, x, y, own)
+        name="local",
+    )(g, y, own)
     return out.reshape(matrix.shape)
 
 

time: 459 us -> 271 us (0.59)
  the two profiles are of different devices: /device:TPU:160 before, /device:TPU:17 now
where the time goes in v2:
time: 271 us
  Pallas kernels  261 us (96%)
  local copies, waits for them, and re-layouts  5.25 us (2%)
  other arithmetic  4.28 us (2%)
    pallas_call x1, Pallas kernels, on_device(): pl.pallas_call(gather_entry, out_shape=[jax.ShapeDtypeStruct((STEPS, SLOT...  135 us
    pallas_call x1, Pallas kernels, on_device(): pl.pallas_call(local_entry, out_shape=jax.ShapeDtypeStruct((2, B, 2 * B),...  126 us

profile of v2, /device:TPU:17, one launch (start us, length us, event | category | flops | bytes accessed | tf_op | source)
XLA Modules:
  0.0 271.0 jit_solution(15648102019940830510)
XLA Ops:
  0.0 4.3 %reduce = f32[2,256,2,256]{3,2,1,0:T(2,128)S(1)} reduce(f32[2,1,256,2,1,256]{5,4,3,2,1,0:T(1,128)} %param.1, f32[]{:T(128)} %constant.1), dimensions={1,4}, to_apply=%param.1.reduce_sub_computation | reduce | bytes 2097156 | tf_op args[0]
  4.3 1.8 reshape.6.own.own_ref
  6.1 135.5 %gather.1 = (f32[8,10,256,256]{3,2,1,0:T(8,128)}, f32[8,256,512]{2,1,0:T(8,128)}) custom-call(f32[2,256,512]{2,1,0:T(8,128)} %reshape.6.own.own_ref), custom_call_target="tpu_custom_call" | custom-call | tf_op jit(solution)/shard_map/gather/pallas_call | solution.py:422
  141.6 126.0 %local.1 = f32[2,256,512]{2,1,0:T(8,128)} custom-call(f32[8,10,256,256]{3,2,1,0:T(8,128)} %get-tuple-element.7.g_in, f32[8,256,512]{2,1,0:T(8,128)} %get-tuple-element.8.y_in, f32[2,256,512]{2,1,0:T(8,128)} %reshape.6.own.own_ref), custom_call_target="tpu_custom_call" | custom-call | tf_op jit(solution)/shard_map/local/pallas_call | solution.py:432
  267.6 3.4 %reshape.8 = f32[2,1,256,2,1,256]{5,4,3,2,1,0:T(1,128)} reshape(f32[2,256,512]{2,1,0:T(8,128)} %local.1) | data formatting | bytes 2097152 | tf_op jit(solution)/shard_map/reshape | solution.py:441

commit v3 on v2

--- a/solution.py
+++ b/solution.py
@@ -120,24 +120,8 @@
 def nn3(ah, al, bh, bl):
     return nn(ah, bh) + nn(ah, bl) + nn(al, bh)
 
-def local_kernel(p, q, g_in, y_in, own_ref, out_ref,
-                 g, lh, ll, uh, ul, y, tb, ud, lb, zpad, wh, wl, held, g_sem, y_sem):
-    def slot_of(i):
-        return jnp.where((i == p) & (i < STEPS), STEPS, i)
-
-    for k in range(STEPS):
-        for i in range(k, SLOTS):
-            pltpu.make_async_copy(g_in.at[k, slot_of(i)], g.at[k, i], g_sem.at[k, i]).start()
-        pltpu.make_async_copy(y_in.at[k], y.at[k], y_sem.at[k]).start()
-    out_ref[...] = own_ref[...]
-
+def compute(p, q, g, y, out_ref, lh, ll, uh, ul, tb, ud, lb, zpad, wh, wl, held):
     def step(k, _):
-        def arrive(i, _):
-            pltpu.make_async_copy(g_in.at[k, i], g.at[k, i], g_sem.at[k, i]).wait()
-            return 0
-        lax.fori_loop(k, SLOTS, arrive, 0)
-        pltpu.make_async_copy(y_in.at[k], y.at[k], y_sem.at[k]).wait()
-
         def pair(r):
             return pl.ds(2 * r, 2)
 
@@ -205,11 +189,10 @@
 
 def scratch():
     V = pltpu.VMEM
-    return [V((STEPS, SLOTS, B, B), F32), V((STEPS, SLOTS, B, B), BF16), V((STEPS, SLOTS, B, B), BF16),
-            V((STEPS, B, 2 * B), BF16), V((STEPS, B, 2 * B), BF16), V((STEPS, B, 2 * B), F32),
+    return [V((STEPS, SLOTS, B, B), BF16), V((STEPS, SLOTS, B, B), BF16),
+            V((STEPS, B, 2 * B), BF16), V((STEPS, B, 2 * B), BF16),
             V((4, 4, 64, 128), F32), V((4, 64, 128), F32), V((4, 4, 64, 128), F32), V((320, B), F32),
-            V((B, B), BF16), V((B, B), BF16), V((2, B, B), F32),
-            pltpu.SemaphoreType.DMA((STEPS, SLOTS)), pltpu.SemaphoreType.DMA((STEPS,))]
+            V((B, B), BF16), V((B, B), BF16), V((2, B, B), F32)]
 MESH = pl.DeviceIdType.MESH
 
 class Comm:
@@ -398,46 +381,34 @@
 from jax.sharding import PartitionSpec as P
 
 
-def gather_entry(own, g_out, y_out, g, y, out_sem, *sems):
+def entry(own, out_ref, g, y, own_sem, *rest):
     p, q = lax.axis_index("row"), lax.axis_index("col")
-    Comm(p, q, own, g, y, *sems).run()
-    outs = [pltpu.make_async_copy(y, y_out, out_sem.at[0])]
-    for k in range(8):
-        outs.append(pltpu.make_async_copy(g.at[k, pl.ds(k, 10 - k)], g_out.at[k, pl.ds(k, 10 - k)], out_sem.at[1 + k]))
-
+    n = len(comm_scratch())
+    mine = pltpu.make_async_copy(own, out_ref, own_sem)
+    mine.start()
+    Comm(p, q, own, g, y, *rest[:n]).run()
+    mine.wait()
     row = jnp.minimum(p, 7)
-    for c in outs:
-        c.start()
-    for c in outs:
-        c.wait()
-
-
-def local_entry(g_in, y_in, own_ref, out_ref, *rest):
-    local_kernel(lax.axis_index("row"), lax.axis_index("col"), g_in, y_in, own_ref, out_ref, *rest)
+
+    def fill(k, _):
+        g[k, row] = g[k, 8]
+        return 0
+    lax.fori_loop(0, jnp.where(p < 8, p + 1, 0), fill, 0)
+    compute(p, q, g, y, out_ref, *rest[n:])
 
 
 def on_device(matrix):
     own = matrix.reshape(2, B, 2 * B)
-    any_spec = pl.BlockSpec(memory_space=pl.ANY)
-    g, y = pl.pallas_call(
-        gather_entry,
-        out_shape=[jax.ShapeDtypeStruct((STEPS, SLOTS, B, B), F32), jax.ShapeDtypeStruct((STEPS, B, 2 * B), F32)],
-        in_specs=[any_spec],
-        out_specs=[any_spec] * 2,
+    out = pl.pallas_call(
+        entry,
+        out_shape=jax.ShapeDtypeStruct((2, B, 2 * B), F32),
+        in_specs=[pl.BlockSpec(memory_space=pl.ANY)],
+        out_specs=pl.BlockSpec(memory_space=pltpu.VMEM),
         scratch_shapes=[pltpu.VMEM((STEPS, SLOTS, B, B), F32), pltpu.VMEM((STEPS, B, 2 * B), F32),
-                        pltpu.SemaphoreType.DMA((9,))] + comm_scratch(),
+                        pltpu.SemaphoreType.DMA] + comm_scratch() + scratch(),
         compiler_params=pltpu.CompilerParams(vmem_limit_bytes=63 * 1024 * 1024, collective_id=0, has_side_effects=True),
-        name="gather",
+        name="steps",
     )(own)
-    out = pl.pallas_call(
-        local_entry,
-        out_shape=jax.ShapeDtypeStruct((2, B, 2 * B), F32),
-        in_specs=[any_spec] * 2 + [pl.BlockSpec(memory_space=pltpu.VMEM)],
-        out_specs=pl.BlockSpec(memory_space=pltpu.VMEM),
-        scratch_shapes=scratch(),
-        compiler_params=pltpu.CompilerParams(vmem_limit_bytes=63 * 1024 * 1024),
-        name="local",
-    )(g, y, own)
     return out.reshape(matrix.shape)
 
 

time: 271 us -> 258 us (0.952)
  Pallas kernels: 261 us -> 249 us
    pallas_call x2 -> x1, Pallas kernels: 261 us -> 249 us  [on_device(): pl.pallas_call(entry, out_shape=jax.ShapeDtypeStruct((2, B, 2 * B), F32),...]
where the time goes in v3:
time: 258 us
  Pallas kernels  249 us (97%)
  local copies, waits for them, and re-layouts  5.25 us (2%)
  other arithmetic  4.28 us (2%)
    pallas_call x1, Pallas kernels, on_device(): pl.pallas_call(entry, out_shape=jax.ShapeDtypeStruct((2, B, 2 * B), F32),...  249 us

profile of v3, /device:TPU:17, one launch (start us, length us, event | category | flops | bytes accessed | tf_op | source)
XLA Modules:
  0.0 258.2 jit_solution(17556364507655992111)
XLA Ops:
  0.0 4.3 %reduce = f32[2,256,2,256]{3,2,1,0:T(2,128)S(1)} reduce(f32[2,1,256,2,1,256]{5,4,3,2,1,0:T(1,128)} %param.1, f32[]{:T(128)} %constant.1), dimensions={1,4}, to_apply=%param.1.reduce_sub_computation | reduce | bytes 2097156 | tf_op args[0]
  4.3 1.8 reshape.6.own
  6.1 248.6 %steps.1 = f32[2,256,512]{2,1,0:T(8,128)} custom-call(f32[2,256,512]{2,1,0:T(8,128)} %reshape.6.own), custom_call_target="tpu_custom_call" | custom-call | tf_op jit(solution)/shard_map/steps/pallas_call | solution.py:402
  254.7 3.4 %reshape.8 = f32[2,1,256,2,1,256]{5,4,3,2,1,0:T(1,128)} reshape(f32[2,256,512]{2,1,0:T(8,128)} %steps.1) | data formatting | bytes 2097152 | tf_op jit(solution)/shard_map/reshape | solution.py:412

commit v4 on v3

--- a/solution.py
+++ b/solution.py
@@ -49,7 +49,7 @@
 def nn(a, b):
     return lax.dot_general(a, b, (((1,), (0,)), ((), ())), preferred_element_type=F32)
 
-def factor_tile(tb, ud, lb, zpad, w_hi, w_lo):
+def factor_tile(tb, ud, lb, zpad, w_hi, w_lo, before=None, beside=None):
     low = lax.broadcasted_iota(jnp.int32, (64, 128), 1) < 64
     eye = jnp.where(
         lax.broadcasted_iota(jnp.int32, (64, 128), 1)
@@ -57,6 +57,10 @@
     zpad[...] = jnp.zeros_like(zpad)
 
     def group(g, _):
+        if before is not None:
+            before(g)
+        if beside is not None:
+            beside(g)
         block = jnp.where(low, tb[g, g], eye)
         done = eliminate([block[8 * i:8 * i + 8] for i in range(8)])
         m = jnp.concatenate(done, 0)
@@ -120,41 +124,42 @@
 def nn3(ah, al, bh, bl):
     return nn(ah, bh) + nn(ah, bl) + nn(al, bh)
 
-def compute(p, q, g, y, out_ref, lh, ll, uh, ul, tb, ud, lb, zpad, wh, wl, held):
+def pair(r):
+    return pl.ds(2 * r, 2)
+
+def lead_factor(p, q, g, lh, ll, wh, wl, tb, ud, lb, zpad, held, ready, pump):
+    def apply(j, r, m):
+        got = nt3(lh[m, pair(r)].reshape(512, B), ll[m, pair(r)].reshape(512, B), lh[m, j], ll[m, j])
+        g[j, pair(r)] = g[j, pair(r)] - got.reshape(2, B, B)
+
     def step(k, _):
-        def pair(r):
-            return pl.ds(2 * r, 2)
-
-        def update(r, _):
-            def term(m, _):
-                got = nt3(lh[m, pair(r)].reshape(512, B), ll[m, pair(r)].reshape(512, B), lh[m, k], ll[m, k])
-                g[k, pair(r)] = g[k, pair(r)] - got.reshape(2, B, B)
-                return 0
-            return lax.fori_loop(0, k, term, 0)
-        lax.fori_loop(k // 2, 5, update, 0)
-
+        ready(k)
+
+        def last(r, _):
+            apply(k, r, k - 1)
+            return 0
+        lax.fori_loop(jnp.where(k > 0, k // 2, 4), 4, last, 0)
         blocks(g[k, k], tb)
-        factor_tile(tb, ud, lb, zpad, wh, wl)
+
+        def beside(i):
+            j = k + 1
+            rows = jnp.maximum(4 - j // 2, 1)
+            for n in range(2):
+                turn = 2 * i + n
+                m = turn // rows
+                on = (m < k) & (j < STEPS)
+                apply(jnp.where(on, j, 7), jnp.where(on, j // 2 + turn % rows, 0), jnp.where(on, m, 0))
+
+        factor_tile(tb, ud, lb, zpad, wh.at[k], wl.at[k], lambda i: pump(4 * k + i), beside)
 
         def solve(r, _):
             ah, al = split(g[k, pair(r)].reshape(512, B))
-            got = nt3(ah, al, wh[...], wl[...]).reshape(2, B, B)
+            got = nt3(ah, al, wh[k], wl[k]).reshape(2, B, B)
             hi, lo = split(got)
             lh[k, pair(r)] = hi
             ll[k, pair(r)] = lo
             return 0
         lax.fori_loop(k // 2, 4, solve, 0)
-
-        ah, al = split(g[k, 8:10].reshape(512, B))
-        got = nt3(ah, al, wh[...], wl[...])
-        got = jnp.concatenate([jnp.where(p > k, got[:B], 0.0), got[B:]], 0)
-        hi, lo = split(got)
-        lh[k, 8:10] = hi.reshape(2, B, B)
-        ll[k, 8:10] = lo.reshape(2, B, B)
-
-        @pl.when(q == k)
-        def _():
-            held[...] = got.reshape(2, B, B)
 
         @pl.when((q == k) & (p == k))
         def _():
@@ -167,19 +172,42 @@
                 parts = [lb[i, j] if j < i else (twice if j == i else jnp.zeros((64, 128), F32)) for j in range(4)]
                 for h in range(2):
                     held[0, 64 * i:64 * i + 64, 128 * h:128 * h + 128] = jnp.where(low, parts[2 * h], parts[2 * h + 1])
-
-        def uterm(m, _):
-            y[k] = y[k] - nn3(lh[m, k], ll[m, k], uh[m], ul[m])
+        return 0
+    lax.fori_loop(0, STEPS, step, 0)
+
+def own_panels(p, q, g, y, out_ref, lh, ll, wh, wl, held):
+    def step(k, _):
+        ah, al = split(g[k, 8:10].reshape(512, B))
+        left = nt3(ah, al, wh[k], wl[k])
+        left = jnp.concatenate([jnp.where(p > k, left[:B], 0.0), left[B:]], 0)
+        xh, xl = split(left)
+        yh, yl = split(y[k])
+        up = nn3(wh[k], wl[k], yh, yl)
+        up = jnp.concatenate([jnp.where(q > k, up[:, :B], 0.0), up[:, B:]], 1)
+        uh, ul = split(up)
+        lh[k, 8:10] = xh.reshape(2, B, B)
+        ll[k, 8:10] = xl.reshape(2, B, B)
+        y[k] = up
+
+        @pl.when((q == k) & (p != k))
+        def _():
+            held[0] = left[:B]
+
+        @pl.when(q == k)
+        def _():
+            held[1] = left[B:]
+
+        for a in range(2):
+            out_ref[a] = out_ref[a] - nn3(xh[B * a:B * a + B], xl[B * a:B * a + B], uh, ul)
+
+        def later(j, _):
+            xh = lh[k, 8:10].reshape(512, B)
+            xl = ll[k, 8:10].reshape(512, B)
+            uh, ul = split(y[k])
+            g[j, 8:10] = g[j, 8:10] - nt3(xh, xl, lh[k, j], ll[k, j]).reshape(2, B, B)
+            y[j] = y[j] - nn3(lh[k, j], ll[k, j], uh, ul)
             return 0
-        lax.fori_loop(0, k, uterm, 0)
-        yh, yl = split(y[k])
-        u = nn3(wh[...], wl[...], yh, yl)
-        u = jnp.concatenate([jnp.where(q > k, u[:, :B], 0.0), u[:, B:]], 1)
-        hi, lo = split(u)
-        uh[k] = hi
-        ul[k] = lo
-        for a in range(2):
-            out_ref[a] = out_ref[a] - nn3(lh[k, 8 + a], ll[k, 8 + a], hi, lo)
+        lax.fori_loop(k + 1, STEPS, later, 0)
         return 0
     lax.fori_loop(0, STEPS, step, 0)
 
@@ -190,9 +218,9 @@
 def scratch():
     V = pltpu.VMEM
     return [V((STEPS, SLOTS, B, B), BF16), V((STEPS, SLOTS, B, B), BF16),
-            V((STEPS, B, 2 * B), BF16), V((STEPS, B, 2 * B), BF16),
+            V((STEPS, B, B), BF16), V((STEPS, B, B), BF16),
             V((4, 4, 64, 128), F32), V((4, 64, 128), F32), V((4, 4, 64, 128), F32), V((320, B), F32),
-            V((B, B), BF16), V((B, B), BF16), V((2, B, B), F32)]
+            V((2, B, B), F32)]
 MESH = pl.DeviceIdType.MESH
 
 class Comm:
@@ -201,7 +229,7 @@
         self.px, self.py, self.pz, self.c = p % 4, p // 4, q // 2, q % 2
         self.send_sem, self.g_sem, self.y_sem = send_sem, g_sem, y_sem
         self.x_sem, self.d_sem, self.own_sem = x_sem, d_sem, own_sem
-        self.sent = []
+        self.base, self.next, self.waiting = self.layout()[0], 0, False
 
     def at_z(self, d):
         return (self.p, 2 * ((self.pz + d) % 8) + self.c)
@@ -223,19 +251,48 @@
         pl.semaphore_wait(b, len(peers))
 
     def send(self, cond, src, dst, sem, to):
-        c = pltpu.make_async_remote_copy(src_ref=src, dst_ref=dst, send_sem=self.send_sem.at[len(self.sent)],
+        c = pltpu.make_async_remote_copy(src_ref=src, dst_ref=dst, send_sem=self.send_sem.at[self.next],
                                          recv_sem=sem, device_id=to, device_id_type=MESH)
-        pl.when(cond)(c.start)
-        self.sent.append((cond, c))
+        self.next += 1
+        pl.when(cond)(c.wait_send if self.waiting else c.start)
 
     def take(self, cond, ref, sem):
+        if self.waiting:
+            return
         c = pltpu.make_async_remote_copy(src_ref=ref, dst_ref=ref, send_sem=self.send_sem.at[0],
                                          recv_sem=sem, device_id=self.sibling(), device_id_type=MESH)
         pl.when(cond)(c.wait_recv)
 
-    def drain(self):
-        for cond, c in self.sent:
-            pl.when(cond)(c.wait_send)
+    @staticmethod
+    def count(name, args):
+        if name == "z_hop":
+            return 4 * (3 if args[1] == 0 else 1)
+        if name == "y_own":
+            return 8
+        if name in ("y_forward", "x_sibling"):
+            return 4
+        rows = len(args[1]) if len(args) > 1 else 2
+        tile = args[0] is not None
+        return rows * {"x_send": 8 + tile, "x_forward": 4, "finish": 3 * tile}[name]
+
+    @classmethod
+    def layout(cls):
+        every = list(cls.BEGIN) + [op for n in sorted(cls.SCHEDULE) for op in cls.SCHEDULE[n]]
+        base, at = {}, 0
+        for name, *args in every:
+            base[name, tuple(args)] = at
+            at += cls.count(name, args)
+        return base, at
+
+    def do(self, name, *args):
+        self.next = self.base[name, args]
+        getattr(self, name)(*args)
+        assert self.next <= self.base[name, args] + self.count(name, args), (name, args)
+
+    def drain(self, name, *args):
+        self.waiting = True
+        self.do(name, *args)
+        self.waiting = False
 
     def local(self):
         p, q = self.p, self.q
@@ -248,12 +305,12 @@
     def gp(self, k, slot, piece):
         return self.g.at[k, slot, pl.ds(64 * piece, 64)]
 
-    def z_hop(self, s):
+    def z_hop(self, s, a):
         for d, pieces in ((1, (0, 1)), (-1, (2, 3))):
             zs = (self.pz - d * s) % 8
             on = zs < 4
             k = jnp.minimum(2 * zs + self.c, 7)
-            for a in range(2):
+            if True:
                 for piece in pieces:
                     ref, sem = self.gp(k, 8 + a, piece), self.g_sem.at[k, 8 + a, piece]
                     if s > 0:
@@ -273,7 +330,8 @@
             for e in (1, -1):
                 self.send(self.p < 8, ref, ref, self.y_sem.at[pp, piece], self.at_y(e))
 
-    def item(self, k):
+    def item(self, i):
+        k = None if i is None else 2 * i + self.c
         if k is None:
             ref = lambda r, piece: self.y.at[r, pl.ds(64 * piece, 64)]
             return ref, ref, (lambda r, piece: self.y_sem.at[r, piece]), (lambda r: True)
@@ -284,6 +342,7 @@
 
     def y_forward(self, k):
         src, dst, sem, has = self.item(k)
+        k = None if k is None else 2 * k + self.c
         for d, pieces in ((1, (0, 1)), (-1, (2, 3))):
             ys = (self.py - d) % 4
             r = jnp.minimum(4 * ys + self.px, 7)
@@ -292,9 +351,10 @@
                 self.take(on, dst(r, piece), sem(r, piece))
                 self.send(on, dst(r, piece), dst(r, piece), sem(r, piece), self.at_y(d))
 
-    def x_send(self, k):
+    def x_send(self, k, rows=(0, 1)):
         src, dst, sem, has = self.item(k)
-        for ys in range(2):
+        k = None if k is None else 2 * k + self.c
+        for ys in rows:
             r = 4 * ys + self.px
             dist = (self.py - ys) % 4
             for piece in range(4):
@@ -305,78 +365,116 @@
             if k is not None:
                 self.send(has(r) & (dist != 0), self.g.at[k, r], self.g.at[k, r], self.d_sem.at[k, r], self.sibling())
 
-    def x_forward(self, k):
+    def x_forward(self, k, rows=(0, 1)):
         src, dst, sem, has = self.item(k)
+        k = None if k is None else 2 * k + self.c
         for d, pieces in ((1, (0, 1)), (-1, (2, 3))):
             xs = (self.px - d) % 4
-            for ys in range(2):
+            for ys in rows:
                 r = 4 * ys + xs
                 for piece in pieces:
                     self.take(jnp.bool_(True) & has(r), dst(r, piece), sem(r, piece))
                     self.send(jnp.bool_(True) & has(r), dst(r, piece), dst(r, piece), sem(r, piece), self.at_x(d))
 
-    def finish(self, k):
+    def finish(self, k, rows=(0, 1)):
         src, dst, sem, has = self.item(k)
+        k = None if k is None else 2 * k + self.c
         for dx in (1, 3, 2):
             xs = (self.px - dx) % 4
             pieces = {1: (2, 3), 3: (0, 1), 2: (0, 1, 2, 3)}[dx]
-            for ys in range(2):
+            for ys in rows:
                 r = 4 * ys + xs
                 for piece in pieces:
                     self.take(jnp.bool_(True) & has(r), dst(r, piece), sem(r, piece))
                 if k is not None:
                     self.send(has(r), self.g.at[k, r], self.g.at[k, r], self.d_sem.at[k, r], self.sibling())
 
-    def x_sibling(self):
+    def x_sibling(self, a):
         for i in range(4):
             k = 2 * i + self.c
-            self.send(jnp.bool_(True) & (k < 8), self.g.at[k, pl.ds(8, 2)], self.g.at[k, pl.ds(8, 2)], self.x_sem.at[k], self.sibling())
-
-    def from_sibling(self):
+            self.send(k < 8, self.g.at[k, 8 + a], self.g.at[k, 8 + a], self.x_sem.at[k, a], self.sibling())
+
+    def from_sibling(self, i):
+        k = 2 * i + 1 - self.c
+        self.take(k < 8, self.g.at[k, 8], self.x_sem.at[k, 0])
+        for r in range(8):
+            self.take((k <= r) & (r != self.p), self.g.at[k, r], self.d_sem.at[k, r])
+
+    def from_sibling_late(self):
         for i in range(4):
             k = 2 * i + 1 - self.c
-            self.take(k < 8, self.g.at[k, pl.ds(8, 2)], self.x_sem.at[k])
-            for r in range(8):
-                self.take((k <= r) & (r != self.p), self.g.at[k, r], self.d_sem.at[k, r])
-
-    def run(self):
+            self.take(k < 8, self.g.at[k, 9], self.x_sem.at[k, 1])
+
+    def begin(self):
         mine = self.local()
         for on, c in mine:
             pl.when(on)(c.start)
         self.barrier()
         for on, c in mine:
             pl.when(on)(c.wait)
-        ks = [2 * i + self.c for i in range(4)]
-        self.z_hop(0)
-        self.y_own()
-        self.z_hop(1)
-        self.z_hop(2)
-        self.y_forward(None)
-        self.z_hop(3)
-        self.x_send(None)
-        self.z_hop(4)
-        self.x_forward(None)
-        self.z_hop(5)
-        self.z_hop(6)
-        self.z_hop(7)
-        self.x_sibling()
-        for k in ks:
-            self.y_forward(k)
-        for k in ks:
-            self.x_send(k)
-        for k in ks:
-            self.x_forward(k)
-        for k in ks:
-            self.finish(k)
-        self.finish(None)
-        self.from_sibling()
-        self.drain()
-
-N_SEND = 640
+        for op in self.BEGIN:
+            self.do(*op)
+
+    BEGIN = (
+        [("z_hop", 0, 0), ("y_own",), ("z_hop", 1, 0), ("z_hop", 2, 0), ("y_forward", None), ("x_send", None, (0,))]
+        + [("z_hop", s, 0) for s in range(3, 8)]
+        + [("x_sibling", 0), ("z_hop", 0, 1), ("y_forward", 0), ("x_send", 0), ("y_forward", 1), ("x_forward", 0),
+           ("finish", 0), ("x_send", 1)]
+    )
+
+    SCHEDULE = {
+        0: [("x_forward", 1), ("z_hop", 1, 1)],
+        1: [("finish", 1), ("y_forward", 2)],
+        2: [("x_send", 2), ("z_hop", 2, 1)],
+        3: [("x_forward", 2)],
+        4: [("finish", 2), ("z_hop", 3, 1)],
+        5: [("y_forward", 3), ("x_send", 3)],
+        6: [("z_hop", 4, 1)],
+        7: [("x_forward", 3)],
+        8: [("finish", 3), ("z_hop", 5, 1)],
+        9: [("x_send", None, (1,))],
+        10: [("z_hop", 6, 1)],
+        11: [("x_forward", None, (0,))],
+        12: [("z_hop", 7, 1), ("x_sibling", 1)],
+        13: [("x_forward", None, (1,))],
+        16: [("finish", None)],
+    }
+
+    def pump(self, it):
+        for top in range(0, 20, 4):
+            @pl.when(it // 4 == top // 4)
+            def _():
+                for n in range(top, top + 4):
+                    if n in self.SCHEDULE:
+                        @pl.when(it == n)
+                        def _():
+                            for op in self.SCHEDULE[n]:
+                                self.do(*op)
+
+    def ready(self, k):
+        for i in range(4):
+            @pl.when(k == max(2 * i - 1, 0))
+            def _():
+                self.from_sibling(i)
+                for name in ("y_forward", "x_send", "x_forward", "finish"):
+                    self.drain(name, i)
+                row = jnp.minimum(self.p, 7)
+                for col in (2 * i, 2 * i + 1):
+                    @pl.when((self.p < 8) & (col <= self.p))
+                    def _():
+                        self.g[col, row] = self.g[col, 8]
+
+    def end(self):
+        self.from_sibling_late()
+        done = {(n, (i,)) for n in ("y_forward", "x_send", "x_forward", "finish") for i in range(4)}
+        for name, args in list(self.base):
+            if (name, args) not in done:
+                self.drain(name, *args)
+
 
 def comm_scratch():
     D = pltpu.SemaphoreType.DMA
-    return [D((N_SEND,)), D((8, 10, 4)), D((8, 4)), D((8,)), D((8, 8)), D((3,))]
+    return [D((Comm.layout()[1],)), D((8, 10, 4)), D((8, 4)), D((8, 2)), D((8, 8)), D((3,))]
 
 from jax.sharding import PartitionSpec as P
 
@@ -384,17 +482,15 @@
 def entry(own, out_ref, g, y, own_sem, *rest):
     p, q = lax.axis_index("row"), lax.axis_index("col")
     n = len(comm_scratch())
+    lh, ll, wh, wl, *work, held = rest[n:]
     mine = pltpu.make_async_copy(own, out_ref, own_sem)
     mine.start()
-    Comm(p, q, own, g, y, *rest[:n]).run()
+    comm = Comm(p, q, own, g, y, *rest[:n])
+    comm.begin()
+    lead_factor(p, q, g, lh, ll, wh, wl, *work, held, comm.ready, comm.pump)
     mine.wait()
-    row = jnp.minimum(p, 7)
-
-    def fill(k, _):
-        g[k, row] = g[k, 8]
-        return 0
-    lax.fori_loop(0, jnp.where(p < 8, p + 1, 0), fill, 0)
-    compute(p, q, g, y, out_ref, *rest[n:])
+    comm.end()
+    own_panels(p, q, g, y, out_ref, lh, ll, wh, wl, held)
 
 
 def on_device(matrix):

time: 258 us -> 215 us (0.83)
  the two profiles are of different devices: /device:TPU:17 before, /device:TPU:28 now
where the time goes in v4:
time: 215 us
  Pallas kernels  205 us (95%)
  local copies, waits for them, and re-layouts  5.25 us (2%)
  other arithmetic  4.28 us (2%)
    pallas_call x1, Pallas kernels, on_device(): pl.pallas_call(entry, out_shape=jax.ShapeDtypeStruct((2, B, 2 * B), F32),...  205 us

profile of v4, /device:TPU:28, one launch (start us, length us, event | category | flops | bytes accessed | tf_op | source)
XLA Modules:
  0.0 215.0 jit_solution(2524013598425243541)
XLA Ops:
  0.0 4.3 %reduce = f32[2,256,2,256]{3,2,1,0:T(2,128)S(1)} reduce(f32[2,1,256,2,1,256]{5,4,3,2,1,0:T(1,128)} %param.1, f32[]{:T(128)} %constant.1), dimensions={1,4}, to_apply=%param.1.reduce_sub_computation | reduce | bytes 2097156 | tf_op args[0]
  4.3 1.8 reshape.6.own
  6.1 205.4 %steps.1 = f32[2,256,512]{2,1,0:T(8,128)} custom-call(f32[2,256,512]{2,1,0:T(8,128)} %reshape.6.own), custom_call_target="tpu_custom_call" | custom-call | tf_op jit(solution)/shard_map/steps/pallas_call | solution.py:498
  211.5 3.4 %reshape.8 = f32[2,1,256,2,1,256]{5,4,3,2,1,0:T(1,128)} reshape(f32[2,256,512]{2,1,0:T(8,128)} %steps.1) | data formatting | bytes 2097152 | tf_op jit(solution)/shard_map/reshape | solution.py:508

commit v5 on v4

--- a/solution.py
+++ b/solution.py
@@ -127,7 +127,7 @@
 def pair(r):
     return pl.ds(2 * r, 2)
 
-def lead_factor(p, q, g, lh, ll, wh, wl, tb, ud, lb, zpad, held, ready, pump):
+def lead_factor(p, q, g, lh, ll, wh, wl, tb, ud, lb, zpad, held, ready, ready_rest, pump):
     def apply(j, r, m):
         got = nt3(lh[m, pair(r)].reshape(512, B), ll[m, pair(r)].reshape(512, B), lh[m, j], ll[m, j])
         g[j, pair(r)] = g[j, pair(r)] - got.reshape(2, B, B)
@@ -136,8 +136,10 @@
         ready(k)
 
         def last(r, _):
-            apply(k, r, k - 1)
-            return 0
+            def term(m, _):
+                apply(k, r, m)
+                return 0
+            return lax.fori_loop(jnp.where(k == 2, 0, k - 1), k, term, 0)
         lax.fori_loop(jnp.where(k > 0, k // 2, 4), 4, last, 0)
         blocks(g[k, k], tb)
 
@@ -147,10 +149,11 @@
             for n in range(2):
                 turn = 2 * i + n
                 m = turn // rows
-                on = (m < k) & (j < STEPS)
+                on = (m < k) & (j < STEPS) & (j != 2)
                 apply(jnp.where(on, j, 7), jnp.where(on, j // 2 + turn % rows, 0), jnp.where(on, m, 0))
 
         factor_tile(tb, ud, lb, zpad, wh.at[k], wl.at[k], lambda i: pump(4 * k + i), beside)
+        ready_rest(k)
 
         def solve(r, _):
             ah, al = split(g[k, pair(r)].reshape(512, B))
@@ -175,7 +178,7 @@
         return 0
     lax.fori_loop(0, STEPS, step, 0)
 
-def own_panels(p, q, g, y, out_ref, lh, ll, wh, wl, held):
+def own_panels(p, q, g, y, tiles, out_ref, lh, ll, wh, wl, held):
     def step(k, _):
         ah, al = split(g[k, 8:10].reshape(512, B))
         left = nt3(ah, al, wh[k], wl[k])
@@ -198,7 +201,7 @@
             held[1] = left[B:]
 
         for a in range(2):
-            out_ref[a] = out_ref[a] - nn3(xh[B * a:B * a + B], xl[B * a:B * a + B], uh, ul)
+            tiles[a] = tiles[a] - nn3(xh[B * a:B * a + B], xl[B * a:B * a + B], uh, ul)
 
         def later(j, _):
             xh = lh[k, 8:10].reshape(512, B)
@@ -213,7 +216,10 @@
 
     @pl.when(q < STEPS)
     def _():
-        out_ref[:, :, :B] = held[...]
+        tiles[:, :, :B] = held[...]
+    for a in range(2):
+        for j in range(4):
+            out_ref[pl.ds(4 * B * a + j, B, stride=4), :] = tiles[a, :, 128 * j:128 * j + 128]
 
 def scratch():
     V = pltpu.VMEM
@@ -224,11 +230,11 @@
 MESH = pl.DeviceIdType.MESH
 
 class Comm:
-    def __init__(self, p, q, own, g, y, send_sem, g_sem, y_sem, x_sem, d_sem, own_sem):
+    def __init__(self, p, q, own, g, y, send_sem, g_sem, y_sem, x_sem, d_sem):
         self.p, self.q, self.own, self.g, self.y = p, q, own, g, y
         self.px, self.py, self.pz, self.c = p % 4, p // 4, q // 2, q % 2
         self.send_sem, self.g_sem, self.y_sem = send_sem, g_sem, y_sem
-        self.x_sem, self.d_sem, self.own_sem = x_sem, d_sem, own_sem
+        self.x_sem, self.d_sem = x_sem, d_sem
         self.base, self.next, self.waiting = self.layout()[0], 0, False
 
     def at_z(self, d):
@@ -265,11 +271,13 @@
 
     @staticmethod
     def count(name, args):
-        if name == "z_hop":
-            return 4 * (3 if args[1] == 0 else 1)
+        if name == "z_from":
+            return 16 if args[1] == 0 else 8
+        if name == "x_sibling":
+            return 1
         if name == "y_own":
             return 8
-        if name in ("y_forward", "x_sibling"):
+        if name == "y_forward":
             return 4
         rows = len(args[1]) if len(args) > 1 else 2
         tile = args[0] is not None
@@ -294,34 +302,47 @@
         self.do(name, *args)
         self.waiting = False
 
-    def local(self):
-        p, q = self.p, self.q
-        lead = jnp.minimum(q, 7)
-        rowk = jnp.minimum(p, 7)
-        return [(q < 8, pltpu.make_async_copy(self.own.at[a, :, pl.ds(0, B)], self.g.at[lead, 8 + a], self.own_sem.at[a]))
-                for a in range(2)] + [
-            (p < 8, pltpu.make_async_copy(self.own.at[0], self.y.at[rowk], self.own_sem.at[2]))]
+    def local(self, tiles):
+        def half(a, j):
+            return self.own[pl.ds(4 * B * a + j, B, stride=4), :]
+
+        for a in range(2):
+            for j in range(4):
+                tiles[a, :, 128 * j:128 * j + 128] = half(a, j)
+
+        @pl.when(self.q < 8)
+        def _():
+            k = jnp.minimum(self.q, 7)
+            for a in range(2):
+                for j in range(2):
+                    self.g[k, 8 + a, :, 128 * j:128 * j + 128] = half(a, j)
+
+        @pl.when(self.p < 8)
+        def _():
+            r = jnp.minimum(self.p, 7)
+            for j in range(4):
+                self.y[r, :, 128 * j:128 * j + 128] = half(0, j)
 
     def gp(self, k, slot, piece):
         return self.g.at[k, slot, pl.ds(64 * piece, 64)]
 
-    def z_hop(self, s, a):
-        for d, pieces in ((1, (0, 1)), (-1, (2, 3))):
-            zs = (self.pz - d * s) % 8
-            on = zs < 4
-            k = jnp.minimum(2 * zs + self.c, 7)
-            if True:
-                for piece in pieces:
-                    ref, sem = self.gp(k, 8 + a, piece), self.g_sem.at[k, 8 + a, piece]
-                    if s > 0:
-                        self.take(on, ref, sem)
-                    if s < 7:
-                        self.send(on, ref, ref, sem, self.at_z(d))
-                    if a == 0:
-                        row = on & (self.p < 8) & (k <= self.p)
-                        pp = jnp.minimum(self.p, 7)
-                        for e in (1, -1):
-                            self.send(row, ref, self.gp(k, pp, piece), self.g_sem.at[k, pp, piece], self.at_y(e))
+    def z_from(self, zs, a):
+        dist = (self.pz - zs) % 8
+        k = 2 * zs + self.c
+        for piece in range(4):
+            ref, sem = self.gp(k, 8 + a, piece), self.g_sem.at[k, 8 + a, piece]
+            self.take(dist != 0, ref, sem)
+            self.send(dist < 4, ref, ref, sem, self.at_z(1))
+            self.send((dist == 0) | (dist > 5), ref, ref, sem, self.at_z(-1))
+            if a == 0:
+                row = (self.p < 8) & (k <= self.p)
+                pp = jnp.minimum(self.p, 7)
+                for e in (1, -1):
+                    self.send(row, ref, self.gp(k, pp, piece), self.g_sem.at[k, pp, piece], self.at_y(e))
+
+    def x_sibling(self, zs, a):
+        k = 2 * zs + self.c
+        self.send(k < 8, self.g.at[k, 8 + a], self.g.at[k, 8 + a], self.x_sem.at[k, a], self.sibling())
 
     def y_own(self):
         pp = jnp.minimum(self.p, 7)
@@ -389,15 +410,11 @@
                 if k is not None:
                     self.send(has(r), self.g.at[k, r], self.g.at[k, r], self.d_sem.at[k, r], self.sibling())
 
-    def x_sibling(self, a):
-        for i in range(4):
-            k = 2 * i + self.c
-            self.send(k < 8, self.g.at[k, 8 + a], self.g.at[k, 8 + a], self.x_sem.at[k, a], self.sibling())
-
-    def from_sibling(self, i):
+    def from_sibling(self, i, rows):
         k = 2 * i + 1 - self.c
-        self.take(k < 8, self.g.at[k, 8], self.x_sem.at[k, 0])
-        for r in range(8):
+        if 0 in rows:
+            self.take(k < 8, self.g.at[k, 8], self.x_sem.at[k, 0])
+        for r in rows:
             self.take((k <= r) & (r != self.p), self.g.at[k, r], self.d_sem.at[k, r])
 
     def from_sibling_late(self):
@@ -405,43 +422,37 @@
             k = 2 * i + 1 - self.c
             self.take(k < 8, self.g.at[k, 9], self.x_sem.at[k, 1])
 
-    def begin(self):
-        mine = self.local()
-        for on, c in mine:
-            pl.when(on)(c.start)
+    BEGIN = [("z_from", 0, 0), ("x_sibling", 0, 0), ("y_forward", 0), ("z_from", 1, 0), ("x_send", 0, (0,)),
+             ("x_forward", 0, (0,)), ("x_send", 0, (1,)), ("finish", 0, (0,))]
+
+    SCHEDULE = {
+        0: [("x_forward", 0, (1,)), ("x_sibling", 1, 0)],
+        1: [("finish", 0, (1,)), ("y_forward", 1)],
+        2: [("x_send", 1, (0, 1)), ("z_from", 2, 0)],
+        3: [("x_forward", 1, (0, 1)), ("x_sibling", 2, 0)],
+        4: [("finish", 1, (0, 1)), ("y_forward", 2)],
+        5: [("x_send", 2, (0, 1)), ("z_from", 3, 0)],
+        6: [("x_forward", 2, (0, 1)), ("x_sibling", 3, 0)],
+        7: [("finish", 2, (0, 1))],
+        8: [("y_forward", 3), ("z_from", 0, 1)],
+        9: [("x_send", 3, (0, 1)), ("y_own",)],
+        10: [("x_forward", 3, (0, 1)), ("z_from", 1, 1)],
+        11: [("finish", 3, (0, 1)), ("y_forward", None)],
+        12: [("x_send", None, (0,)), ("z_from", 2, 1)],
+        14: [("x_forward", None, (0,)), ("z_from", 3, 1)],
+        15: [("x_send", None, (1,))],
+        17: [("x_forward", None, (1,)), ("x_sibling", 0, 1), ("x_sibling", 1, 1), ("x_sibling", 2, 1), ("x_sibling", 3, 1)],
+        20: [("finish", None, (0, 1))],
+    }
+
+    def begin(self, tiles):
+        self.local(tiles)
         self.barrier()
-        for on, c in mine:
-            pl.when(on)(c.wait)
         for op in self.BEGIN:
             self.do(*op)
 
-    BEGIN = (
-        [("z_hop", 0, 0), ("y_own",), ("z_hop", 1, 0), ("z_hop", 2, 0), ("y_forward", None), ("x_send", None, (0,))]
-        + [("z_hop", s, 0) for s in range(3, 8)]
-        + [("x_sibling", 0), ("z_hop", 0, 1), ("y_forward", 0), ("x_send", 0), ("y_forward", 1), ("x_forward", 0),
-           ("finish", 0), ("x_send", 1)]
-    )
-
-    SCHEDULE = {
-        0: [("x_forward", 1), ("z_hop", 1, 1)],
-        1: [("finish", 1), ("y_forward", 2)],
-        2: [("x_send", 2), ("z_hop", 2, 1)],
-        3: [("x_forward", 2)],
-        4: [("finish", 2), ("z_hop", 3, 1)],
-        5: [("y_forward", 3), ("x_send", 3)],
-        6: [("z_hop", 4, 1)],
-        7: [("x_forward", 3)],
-        8: [("finish", 3), ("z_hop", 5, 1)],
-        9: [("x_send", None, (1,))],
-        10: [("z_hop", 6, 1)],
-        11: [("x_forward", None, (0,))],
-        12: [("z_hop", 7, 1), ("x_sibling", 1)],
-        13: [("x_forward", None, (1,))],
-        16: [("finish", None)],
-    }
-
     def pump(self, it):
-        for top in range(0, 20, 4):
+        for top in range(0, 24, 4):
             @pl.when(it // 4 == top // 4)
             def _():
                 for n in range(top, top + 4):
@@ -451,60 +462,76 @@
                             for op in self.SCHEDULE[n]:
                                 self.do(*op)
 
+    def plane_ops(self, i):
+        return [op for op in self.base if op[0] in ("y_forward", "x_send", "x_forward", "finish") and op[1][0] == i]
+
+    def fill(self, i):
+        row = jnp.minimum(self.p, 7)
+        for col in (2 * i, 2 * i + 1):
+            @pl.when((self.p < 8) & (col <= self.p))
+            def _():
+                self.g[col, row] = self.g[col, 8]
+
     def ready(self, k):
-        for i in range(4):
-            @pl.when(k == max(2 * i - 1, 0))
+        @pl.when(k == 0)
+        def _():
+            self.from_sibling(0, range(4))
+            self.fill(0)
+
+        @pl.when(k == 1)
+        def _():
+            for name, args in self.plane_ops(0):
+                self.drain(name, *args)
+
+        for i, at in ((1, 2), (2, 3), (3, 5)):
+            @pl.when(k == at)
             def _():
-                self.from_sibling(i)
-                for name in ("y_forward", "x_send", "x_forward", "finish"):
-                    self.drain(name, i)
-                row = jnp.minimum(self.p, 7)
-                for col in (2 * i, 2 * i + 1):
-                    @pl.when((self.p < 8) & (col <= self.p))
-                    def _():
-                        self.g[col, row] = self.g[col, 8]
+                self.from_sibling(i, range(8))
+                self.fill(i)
+                for name, args in self.plane_ops(i):
+                    self.drain(name, *args)
+
+    def ready_rest(self, k):
+        @pl.when(k == 0)
+        def _():
+            self.from_sibling(0, range(4, 8))
 
     def end(self):
         self.from_sibling_late()
-        done = {(n, (i,)) for n in ("y_forward", "x_send", "x_forward", "finish") for i in range(4)}
-        for name, args in list(self.base):
+        done = [op for i in range(4) for op in self.plane_ops(i)]
+        for name, args in self.base:
             if (name, args) not in done:
                 self.drain(name, *args)
 
-
 def comm_scratch():
     D = pltpu.SemaphoreType.DMA
-    return [D((Comm.layout()[1],)), D((8, 10, 4)), D((8, 4)), D((8, 2)), D((8, 8)), D((3,))]
+    return [D((Comm.layout()[1],)), D((8, 10, 4)), D((8, 4)), D((8, 2)), D((8, 8))]
 
 from jax.sharding import PartitionSpec as P
 
 
-def entry(own, out_ref, g, y, own_sem, *rest):
+def entry(own, out_ref, g, y, tiles, *rest):
     p, q = lax.axis_index("row"), lax.axis_index("col")
     n = len(comm_scratch())
     lh, ll, wh, wl, *work, held = rest[n:]
-    mine = pltpu.make_async_copy(own, out_ref, own_sem)
-    mine.start()
     comm = Comm(p, q, own, g, y, *rest[:n])
-    comm.begin()
-    lead_factor(p, q, g, lh, ll, wh, wl, *work, held, comm.ready, comm.pump)
-    mine.wait()
+    comm.begin(tiles)
+    lead_factor(p, q, g, lh, ll, wh, wl, *work, held, comm.ready, comm.ready_rest, comm.pump)
     comm.end()
-    own_panels(p, q, g, y, out_ref, lh, ll, wh, wl, held)
+    own_panels(p, q, g, y, tiles, out_ref, lh, ll, wh, wl, held)
 
 
 def on_device(matrix):
-    own = matrix.reshape(2, B, 2 * B)
     out = pl.pallas_call(
         entry,
-        out_shape=jax.ShapeDtypeStruct((2, B, 2 * B), F32),
-        in_specs=[pl.BlockSpec(memory_space=pl.ANY)],
+        out_shape=jax.ShapeDtypeStruct((8 * B, 128), F32),
+        in_specs=[pl.BlockSpec(memory_space=pltpu.VMEM)],
         out_specs=pl.BlockSpec(memory_space=pltpu.VMEM),
         scratch_shapes=[pltpu.VMEM((STEPS, SLOTS, B, B), F32), pltpu.VMEM((STEPS, B, 2 * B), F32),
-                        pltpu.SemaphoreType.DMA] + comm_scratch() + scratch(),
+                        pltpu.VMEM((2, B, 2 * B), F32)] + comm_scratch() + scratch(),
         compiler_params=pltpu.CompilerParams(vmem_limit_bytes=63 * 1024 * 1024, collective_id=0, has_side_effects=True),
         name="steps",
-    )(own)
+    )(matrix.reshape(8 * B, 128))
     return out.reshape(matrix.shape)
 
 

time: 215 us -> 234 us (1.088)
  the two profiles are of different devices: /device:TPU:28 before, /device:TPU:240 now
where the time goes in v5:
time: 234 us
  Pallas kernels  231 us (99%)
  local copies, waits for them, and re-layouts  2.91 us (1%)
    pallas_call x1, Pallas kernels, on_device(): pl.pallas_call(entry, out_shape=jax.ShapeDtypeStruct((8 * B, 128), F32),...  231 us

profile of v5, /device:TPU:240, one launch (start us, length us, event | category | flops | bytes accessed | tf_op | source)
XLA Modules:
  0.0 233.9 jit_solution(13849919684061860282)
XLA Ops:
  0.0 231.0 %steps.1 = f32[2048,128]{1,0:T(8,128)} custom-call(f32[2048,128]{1,0:T(8,128)} %bitcast.3), custom_call_target="tpu_custom_call" | custom-call | tf_op jit(solution)/shard_map/steps/pallas_call | solution.py:525
  231.0 2.9 %copy.4 = f32[2,1,256,2,1,256]{5,4,3,2,1,0:T(1,128)} copy(f32[2,1,256,2,1,256]{5,4,3,2,1,0:T(1,128)} %bitcast.2) | data formatting | bytes 2097152

commit v6 on v5

v6 whole, which is shorter than its diff:
```python
import jax, jax.numpy as jnp, functools
from jax import lax
from jax.experimental import pallas as pl
from jax.experimental.pallas import tpu as pltpu

F32, BF16 = jnp.float32, jnp.bfloat16

def over_lanes(v, c):
    return jnp.broadcast_to(v[:, c:c + 1], (8, 128))

def over_rows(v, r):
    return jnp.broadcast_to(v[r:r + 1, :], (8, 128))

def eliminate(rows):
    sub = lax.broadcasted_iota(jnp.int32, (8, 128), 0)
    rows = list(rows)
    diag = [over_lanes(rows[0], t) for t in range(8)]
    for s in range(8):
        off = {i: [over_lanes(rows[i], 8 * s + m) for m in range(8)] for i in range(s + 1, 8)}
        nxt = [over_lanes(rows[s + 1], 8 * (s + 1) + t) for t in range(8)] if s < 7 else None
        top = rows[s]
        for m in range(8):
            root = lax.rsqrt(over_rows(diag[m], m))
            lead = diag[m] * root
            unit = over_rows(top, m) * root
            top = jnp.where(sub == m, unit, top - jnp.where(sub > m, lead, 0.0) * unit)
            scal = {t: over_rows(lead, t) for t in range(m + 1, 8)}
            for t in range(m + 1, 8):
                diag[t] = diag[t] - lead * scal[t]
            for i in range(s + 1, 8):
                mult = off[i][m] * root
                for t in range(m + 1, 8):
                    off[i][t] = off[i][t] - mult * scal[t]
                rows[i] = rows[i] - mult * unit
                if i == s + 1:
                    for t in range(8):
                        nxt[t] = nxt[t] - mult * over_rows(mult, t)
        rows[s] = top
        diag = nxt
    return rows

def split(x):
    hi = x.astype(BF16)
    return hi, (x - hi.astype(F32)).astype(BF16)

def nt(a, b):
    return lax.dot_general(a, b, (((1,), (1,)), ((), ())), preferred_element_type=F32)

def nn(a, b):
    return lax.dot_general(a, b, (((1,), (0,)), ((), ())), preferred_element_type=F32)

def factor_tile(tb, ud, lb, zpad, w_hi, w_lo, before=None, beside=None):
    low = lax.broadcasted_iota(jnp.int32, (64, 128), 1) < 64
    eye = jnp.where(
        lax.broadcasted_iota(jnp.int32, (64, 128), 1)
        == lax.broadcasted_iota(jnp.int32, (64, 128), 0) + 64, 1.0, 0.0).astype(F32)
    zpad[...] = jnp.zeros_like(zpad)

    def group(g, _):
        if before is not None:
            before(g)
        if beside is not None:
            beside(g)
        block = jnp.where(low, tb[g, g], eye)
        done = eliminate([block[8 * i:8 * i + 8] for i in range(8)])
        m = jnp.concatenate(done, 0)
        ud[g] = m
        wz = jnp.where(low, 0.0, m)
        wz_hi, wz_lo = split(wz)
        tcol = tb[:, g].reshape(256, 128)
        t_hi, t_lo = split(tcol)
        w2_hi = jnp.concatenate([wz_hi, wz_hi], 0)
        w2_lo = jnp.concatenate([wz_lo, wz_lo], 0)
        p = nt(jnp.concatenate([t_hi, t_lo], 1), jnp.concatenate([w2_hi, w2_hi], 1)) + nt(t_hi, w2_lo)
        rowblk = lax.broadcasted_iota(jnp.int32, (256, 128), 0) // 64
        p = jnp.where(rowblk > g, p, 0.0)
        lb[:, g] = p.reshape(4, 64, 128)
        hi = p.astype(BF16)
        hif = hi.astype(F32)
        lof = p - hif
        lo = lof.astype(BF16)
        lowp = lax.broadcasted_iota(jnp.int32, (256, 128), 1) < 64
        lhs = jnp.concatenate([jnp.where(lowp, hif, lof).astype(BF16),
                               jnp.where(lowp, hif, 0.0).astype(BF16)], 1)
        for h in range(2):
            parts = []
            for j in (2 * h, 2 * h + 1):
                pj = jnp.concatenate([hi[64 * j:64 * j + 64], lo[64 * j:64 * j + 64]], 1)
                parts += [pj, pj]
            upd = nt(lhs, jnp.concatenate(parts, 0))
            for j in range(2):
                tb[:, 2 * h + j] = tb[:, 2 * h + j] - upd[:, 128 * j:128 * j + 128].reshape(4, 64, 128)
        z = zpad[pl.ds(pl.multiple_of(64 * g, 64), 128), :]
        z_hi, z_lo = split(z)
        mix = nn(jnp.concatenate([wz_hi, wz_lo], 1), jnp.concatenate([z_hi, z_hi], 0)) + nn(wz_hi, z_lo)
        turned = pltpu.roll(m, 64, 1)
        both = jnp.where(low, turned, m)
        here = lax.broadcasted_iota(jnp.int32, (64, 256), 1) // 64 == g
        wrow = jnp.where(here, jnp.concatenate([both, both], 1), -mix)
        at = pl.ds(pl.multiple_of(64 * g, 64), 64)
        r_hi, r_lo = split(wrow)
        w_hi[at, :] = r_hi
        w_lo[at, :] = r_lo
        zpad[64:, :] = zpad[64:, :] + nn(lhs, jnp.concatenate([r_hi, r_hi, r_lo, r_lo], 0))
        return 0
    lax.fori_loop(0, 4, group, 0)

def blocks(tile, tb):
    low = lax.broadcasted_iota(jnp.int32, (256, 128), 1) < 64
    for h in range(2):
        x = tile[:, 128 * h:128 * h + 128]
        r = pltpu.roll(x, 64, 1)
        tb[:, 2 * h] = jnp.where(low, x, r).reshape(4, 64, 128)
        tb[:, 2 * h + 1] = jnp.where(low, r, x).reshape(4, 64, 128)


B = 256
STEPS = 8
SLOTS = 10

def nt3(ah, al, bh, bl):
    return nt(ah, bh) + nt(ah, bl) + nt(al, bh)

def nn3(ah, al, bh, bl):
    return nn(ah, bh) + nn(ah, bl) + nn(al, bh)

def pair(r):
    return pl.ds(2 * r, 2)

def lead_factor(p, g, lx, lh, ll, wh, wl, tb, ud, lb, zpad, ready, ready_rest, pump):
    def apply(j, r, m):
        got = nt3(lh[m, pair(r)].reshape(512, B), ll[m, pair(r)].reshape(512, B), lh[m, j], ll[m, j])
        g[j, pair(r)] = g[j, pair(r)] - got.reshape(2, B, B)

    def step(k, _):
        ready(k)

        def last(r, _):
            def term(m, _):
                apply(k, r, m)
                return 0
            return lax.fori_loop(jnp.where(k == 2, 0, k - 1), k, term, 0)
        lax.fori_loop(jnp.where(k > 0, k // 2, 5), 5, last, 0)
        blocks(g[k, k], tb)

        def beside(i):
            j = k + 1
            rows = jnp.maximum(5 - j // 2, 1)
            for n in range(3):
                turn = 3 * i + n
                m = turn // rows
                on = (m < k) & (j < STEPS) & (j != 2)
                apply(jnp.where(on, j, 7), jnp.where(on, j // 2 + turn % rows, 0), jnp.where(on, m, 0))

        factor_tile(tb, ud, lb, zpad, wh, wl, lambda i: pump(k, i), beside)
        ready_rest(k)

        def solve(r):
            ah, al = split(g[k, pair(r)].reshape(512, B))
            return nt3(ah, al, wh[...], wl[...])

        def keep(r, got):
            hi, lo = split(got.reshape(2, B, B))
            lh[k, pair(r)] = hi
            ll[k, pair(r)] = lo

        got = solve(4)
        got = jnp.concatenate([jnp.where(p > k, got[:B], 0.0), got[B:]], 0)
        keep(4, got)
        lx[k] = got.reshape(2, B, B)

        @pl.when(p == k)
        def _():
            low = lax.broadcasted_iota(jnp.int32, (64, 128), 1) < 64
            tri = lax.broadcasted_iota(jnp.int32, (64, 128), 0) <= lax.broadcasted_iota(jnp.int32, (64, 128), 1)
            for i in range(4):
                up = jnp.where(tri & low, ud[i], 0.0)
                turned = jnp.concatenate([up, jnp.zeros((64, 128), F32)], 0).T[:64]
                twice = turned + pltpu.roll(turned, 64, 1)
                parts = [lb[i, j] if j < i else (twice if j == i else jnp.zeros((64, 128), F32)) for j in range(4)]
                for h in range(2):
                    lx[k, 0, 64 * i:64 * i + 64, 128 * h:128 * h + 128] = jnp.where(low, parts[2 * h], parts[2 * h + 1])

        def rest(r, _):
            keep(r, solve(r))
            return 0
        lax.fori_loop(k // 2, 4, rest, 0)
        return 0
    lax.fori_loop(0, STEPS, step, 0)

def trail(p, q, k, lx, ly, tiles):
    def rows(ref, first):
        t = ref[k].reshape(512, B)
        return split(jnp.concatenate([jnp.where(first > k, t[:B], 0.0), t[B:]], 0))
    xh, xl = rows(lx, p)
    yh, yl = rows(ly, q)
    for a in range(2):
        tiles[a] = tiles[a] - nt3(xh[B * a:B * a + B], xl[B * a:B * a + B], yh, yl)

def put_out(q, lx, tiles, out_ref):
    @pl.when(q < STEPS)
    def _():
        tiles[:, :, :B] = lx[jnp.minimum(q, STEPS - 1)]
    for a in range(2):
        for j in range(4):
            out_ref[pl.ds(4 * B * a + j, B, stride=4), :] = tiles[a, :, 128 * j:128 * j + 128]

def scratch():
    V = pltpu.VMEM
    return [V((STEPS, SLOTS, B, B), BF16), V((STEPS, SLOTS, B, B), BF16), V((B, B), BF16), V((B, B), BF16),
            V((4, 4, 64, 128), F32), V((4, 64, 128), F32), V((4, 4, 64, 128), F32), V((320, B), F32)]
MESH = pl.DeviceIdType.MESH
HOME = 1

class Comm:
    def __init__(self, p, q, own, g, lx, ly, send_sem, g_sem, x_sem, d_sem, in_sem, out_sem, z_sem, s_sem, y_sem):
        self.p, self.q, self.own, self.g, self.lx, self.ly = p, q, own, g, lx, ly
        self.px, self.py, self.pz, self.c = p % 4, p // 4, q // 2, q % 2
        self.send_sem, self.g_sem, self.x_sem, self.d_sem = send_sem, g_sem, x_sem, d_sem
        self.in_sem, self.out_sem = in_sem, out_sem
        self.z_sem, self.s_sem, self.y_sem = z_sem, s_sem, y_sem
        self.base, self.next, self.waiting = self.layout()[0], 0, False
        self.home = self.pz == HOME

    def at_z(self, d):
        return (self.p, 2 * ((self.pz + d) % 8) + self.c)

    def at_y(self, d):
        return (4 * ((self.py + d) % 4) + self.px, self.q)

    def at_x(self, d):
        return (4 * self.py + (self.px + d) % 4, self.q)

    def sibling(self):
        return (self.p, 2 * self.pz + 1 - self.c)

    def barrier(self):
        b = pltpu.get_barrier_semaphore()
        peers = [self.at_z(d) for d in (1, -1, 2, -2)] + [self.at_y(1), self.at_y(-1), self.at_x(1), self.at_x(-1), self.sibling()]
        for d in peers:
            pl.semaphore_signal(b, inc=1, device_id=d, device_id_type=MESH)
        pl.semaphore_wait(b, len(peers))

    def copy(self, cond, src, dst, send_sem, recv_sem, to):
        c = pltpu.make_async_remote_copy(src_ref=src, dst_ref=dst, send_sem=send_sem, recv_sem=recv_sem,
                                         device_id=to, device_id_type=MESH)
        pl.when(cond)(c.wait_send if self.waiting else c.start)

    def send(self, cond, src, dst, sem, to):
        self.copy(cond, src, dst, self.send_sem.at[self.next], sem, to)
        self.next += 1

    def take(self, cond, ref, sem):
        if self.waiting:
            return
        c = pltpu.make_async_remote_copy(src_ref=ref, dst_ref=ref, send_sem=self.send_sem.at[0],
                                         recv_sem=sem, device_id=self.sibling(), device_id_type=MESH)
        pl.when(cond)(c.wait_recv)

    @staticmethod
    def count(name, args):
        if name == "arrive":
            return 8 if args[1] == 0 else 0
        if name == "x_sibling":
            return 1
        if name == "y_forward":
            return 4
        return len(args[1]) * {"x_send": 9, "x_forward": 4, "finish": 3}[name]

    @classmethod
    def layout(cls):
        every = list(cls.BEGIN) + [op for n in sorted(cls.SCHEDULE) for op in cls.SCHEDULE[n]]
        base, at = {}, 0
        for name, *args in every:
            base[name, tuple(args)] = at
            at += cls.count(name, args)
        return base, at

    def do(self, name, *args):
        self.next = self.base[name, args]
        getattr(self, name)(*args)
        assert self.next <= self.base[name, args] + self.count(name, args), (name, args)

    def drain(self, name, *args):
        self.waiting = True
        self.do(name, *args)
        self.waiting = False

    def local(self, tiles):
        def half(a, j):
            return self.own[pl.ds(4 * B * a + j, B, stride=4), :]

        for a in range(2):
            for j in range(4):
                tiles[a, :, 128 * j:128 * j + 128] = half(a, j)

        @pl.when(self.q < 8)
        def _():
            k = jnp.minimum(self.q, 7)
            for a in range(2):
                for j in range(2):
                    self.g[k, 8 + a, :, 128 * j:128 * j + 128] = half(a, j)

    def gp(self, k, slot, piece):
        return self.g.at[k, slot, pl.ds(64 * piece, 64)]

    def to_home(self):
        k = jnp.minimum(self.q, 7)
        for a in range(2):
            for piece in range(4):
                ref = self.gp(k, 8 + a, piece)
                self.copy((self.q < 8) & (self.pz != HOME), ref, ref, self.in_sem.at[a, piece],
                          self.g_sem.at[k, 8 + a, piece], (self.p, 2 * HOME + self.c))

    def arrive(self, zs, a):
        k = 2 * zs + self.c
        for piece in range(4):
            ref, sem = self.gp(k, 8 + a, piece), self.g_sem.at[k, 8 + a, piece]
            if zs != HOME:
                self.take(k < 8, ref, sem)
            if a == 0:
                row = (self.p < 8) & (k <= self.p)
                pp = jnp.minimum(self.p, 7)
                for e in (1, -1):
                    self.send(row, ref, self.gp(k, pp, piece), self.g_sem.at[k, pp, piece], self.at_y(e))

    def x_sibling(self, zs, a):
        k = 2 * zs + self.c
        self.send(k < 8, self.g.at[k, 8 + a], self.g.at[k, 8 + a], self.x_sem.at[k, a], self.sibling())

    def y_forward(self, i):
        k = 2 * i + self.c
        for d, pieces in ((1, (0, 1)), (-1, (2, 3))):
            ys = (self.py - d) % 4
            r = jnp.minimum(4 * ys + self.px, 7)
            on = (ys < 2) & (k <= r)
            for piece in pieces:
                ref, sem = self.gp(k, r, piece), self.g_sem.at[k, r, piece]
                self.take(on, ref, sem)
                self.send(on, ref, ref, sem, self.at_y(d))

    def x_send(self, i, rows):
        k = 2 * i + self.c
        for ys in rows:
            r = 4 * ys + self.px
            dist = (self.py - ys) % 4
            for piece in range(4):
                rest = (dist == 2) | (dist == (1 if piece >= 2 else 3))
                ref, sem = self.gp(k, r, piece), self.g_sem.at[k, r, piece]
                self.take(rest & (k <= r), ref, sem)
                for e in (1, -1):
                    self.send(k <= r, self.gp(k, jnp.where(r == self.p, 8, r), piece), ref, sem, self.at_x(e))
            self.send((k <= r) & (dist != 0), self.g.at[k, r], self.g.at[k, r], self.d_sem.at[k, r], self.sibling())

    def x_forward(self, i, rows):
        k = 2 * i + self.c
        for d, pieces in ((1, (0, 1)), (-1, (2, 3))):
            xs = (self.px - d) % 4
            for ys in rows:
                r = 4 * ys + xs
                for piece in pieces:
                    ref, sem = self.gp(k, r, piece), self.g_sem.at[k, r, piece]
                    self.take(k <= r, ref, sem)
                    self.send(k <= r, ref, ref, sem, self.at_x(d))

    def finish(self, i, rows):
        k = 2 * i + self.c
        for dx, pieces in ((1, (2, 3)), (3, (0, 1)), (2, (0, 1, 2, 3))):
            xs = (self.px - dx) % 4
            for ys in rows:
                r = 4 * ys + xs
                for piece in pieces:
                    self.take(k <= r, self.gp(k, r, piece), self.g_sem.at[k, r, piece])
                self.send(k <= r, self.g.at[k, r], self.g.at[k, r], self.d_sem.at[k, r], self.sibling())

    def from_sibling(self, i, rows):
        k = 2 * i + 1 - self.c
        if 0 in rows:
            self.take(k < 8, self.g.at[k, 8], self.x_sem.at[k, 0])
        for r in rows:
            self.take((k <= r) & (r != self.p), self.g.at[k, r], self.d_sem.at[k, r])
        if 7 in rows:
            self.take(k < 8, self.g.at[k, 9], self.x_sem.at[k, 1])

    BEGIN = [("arrive", 0, 0), ("x_sibling", 0, 0), ("y_forward", 0), ("arrive", 1, 0), ("x_send", 0, (0,)),
             ("x_forward", 0, (0,)), ("x_send", 0, (1,)), ("y_forward", 1), ("finish", 0, (0,))]

    SCHEDULE = {
        0: [("x_sibling", 1, 0), ("arrive", 2, 0), ("arrive", 0, 1), ("x_sibling", 0, 1)],
        1: [("x_forward", 0, (1,)), ("x_send", 1, (0,)), ("y_forward", 2)],
        2: [("x_send", 1, (1,))],
        3: [("finish", 0, (1,)), ("x_sibling", 2, 0), ("arrive", 3, 0)],
        4: [("x_forward", 1, (0,)), ("x_send", 2, (0,))],
        5: [("x_forward", 1, (1,)), ("x_send", 2, (1,)), ("y_forward", 3)],
        6: [("x_sibling", 3, 0), ("arrive", 1, 1), ("x_sibling", 1, 1)],
        7: [("finish", 1, (0, 1))],
        8: [("x_forward", 2, (0, 1)), ("x_send", 3, (0, 1))],
        9: [("arrive", 2, 1), ("x_sibling", 2, 1)],
        10: [("arrive", 3, 1), ("x_sibling", 3, 1)],
        11: [("finish", 2, (0, 1))],
        13: [("x_forward", 3, (0, 1))],
        17: [("finish", 3, (0, 1))],
    }

    def begin(self):
        for op in self.BEGIN:
            self.do(*op)

    def pump(self, k, g):
        it = 4 * k + g
        for top in range(0, 20, 4):
            @pl.when(k == top // 4)
            def _():
                for n in range(top, top + 4):
                    if n in self.SCHEDULE:
                        @pl.when(it == n)
                        def _():
                            for op in self.SCHEDULE[n]:
                                self.do(*op)

        @pl.when((g == 0) & (k >= 1))
        def _():
            self.z_pass(k - 1)
            self.source_rest(k - 1)

        @pl.when((g == 1) & (k >= 2))
        def _():
            self.u_pass(k - 2)

        @pl.when((g == 3) & (k >= 3))
        def _():
            self.v_pass(k - 3)

    def fill(self, i):
        row = jnp.minimum(self.p, 7)
        for col in (2 * i, 2 * i + 1):
            @pl.when((self.p < 8) & (col <= self.p))
            def _():
                self.g[col, row] = self.g[col, 8]

    def drain_item(self, i):
        for name, args in self.base:
            if args[0] == i:
                self.drain(name, *args)

    def ready(self, k):
        @pl.when(k == 0)
        def _():
            self.from_sibling(0, range(4))
            self.fill(0)

        for i, at in ((0, 1), (1, 2), (2, 3), (3, 5)):
            @pl.when(k == at)
            def _():
                if i > 0:
                    self.from_sibling(i, range(8))
                    self.fill(i)
                self.drain_item(i)

    def ready_rest(self, k):
        @pl.when(k == 0)
        def _():
            self.from_sibling(0, range(4, 8))

    def z_pass(self, k):
        dist = (self.pz - HOME) % 8
        for n in range(4):
            ref = self.lx.at[k, self.c, pl.ds(64 * n, 64)]
            self.take(dist != 0, ref, self.z_sem.at[k, n])
            self.copy(dist < 4, ref, ref, self.out_sem.at[k, n], self.z_sem.at[k, n], self.at_z(1))
            self.copy((dist == 0) | (dist > 5), ref, ref, self.out_sem.at[k, 4 + n], self.z_sem.at[k, n], self.at_z(-1))
            self.source(k, self.c, n, 0)

    def s_send(self, k):
        ref = self.lx.at[k, self.c]
        self.copy(self.pz != HOME, ref, ref, self.out_sem.at[k, 8], self.s_sem.at[k], self.sibling())

    def s_take(self, k):
        self.take(self.pz != HOME, self.lx.at[k, 1 - self.c], self.s_sem.at[k])

    def plane(self):
        first = self.c == 0
        u = lambda d: (jnp.where(first, 4 * ((self.py + d) % 4) + self.px, 4 * self.py + (self.px + d) % 4), self.q)
        v = lambda d: (jnp.where(first, 4 * self.py + (self.px + d) % 4, 4 * ((self.py + d) % 4) + self.px), self.q)
        y, x = (self.py - self.q // 4) % 4, (self.px - self.q % 4) % 4
        return u, v, jnp.where(first, y, x), jnp.where(first, x, y)

    def part(self, ref, k, a, n):
        return ref.at[k, a, pl.ds(64 * n, 64)]

    def source(self, k, a, n, half):
        u, v, _, _ = self.plane()
        for e, to in enumerate((u(1), u(-1), v(1), v(-1))):
            self.copy(self.p == self.q, self.part(self.lx, k, a, n), self.part(self.ly, k, a, n),
                      self.out_sem.at[k, 9 + 16 * half + 4 * n + e], self.y_sem.at[k, a, n], to)

    def source_rest(self, k):
        for n in range(4):
            self.source(k, 1 - self.c, n, 1)

    def u_pass(self, k):
        u, v, du, dv = self.plane()
        line = (dv == 0) & (du != 0)
        for half in range(2):
            a = self.c if half == 0 else 1 - self.c
            for n in range(4):
                ref, sem = self.part(self.ly, k, a, n), self.y_sem.at[k, a, n]
                self.take(line, ref, sem)
                at = 9 + 12 * half + 3 * n
                self.copy(line, ref, ref, self.out_sem.at[k, at], sem, v(1))
                self.copy(line, ref, ref, self.out_sem.at[k, at + 1], sem, v(-1))
                self.copy(line & (du == (1 if n < 2 else 3)), ref, ref, self.out_sem.at[k, at + 2], sem, u(1 if n < 2 else -1))

    def v_pass(self, k):
        u, v, du, dv = self.plane()
        for half in range(2):
            a = self.c if half == 0 else 1 - self.c
            for n in range(4):
                ref, sem = self.part(self.ly, k, a, n), self.y_sem.at[k, a, n]
                self.take(dv != 0, ref, sem)
                self.copy(dv == (1 if n < 2 else 3), ref, ref, self.out_sem.at[k, 9 + 4 * half + n], sem, v(1 if n < 2 else -1))

        @pl.when((self.p == self.q) & (not self.waiting))
        def _():
            self.ly[k] = self.lx[k]

    def end(self):
        @pl.when(self.home)
        def _():
            for name, args in self.base:
                if args[0] not in (0, 1, 2, 3):
                    self.drain(name, *args)

        self.waiting = True
        self.to_home()

        def one(k, _):
            self.z_pass(k)
            self.s_send(k)
            self.source_rest(k)
            self.u_pass(k)
            self.v_pass(k)
            return 0
        lax.fori_loop(0, STEPS, one, 0)
        self.waiting = False

def comm_scratch():
    D = pltpu.SemaphoreType.DMA
    return [D((Comm.layout()[1],)), D((8, 10, 4)), D((8, 2)), D((8, 8)), D((2, 4)), D((8, 41)), D((8, 4)), D((8,)), D((8, 2, 4))]

from jax.sharding import PartitionSpec as P


def entry(own, out_ref, g, lx, ly, tiles, *rest):
    p, q = lax.axis_index("row"), lax.axis_index("col")
    n = len(comm_scratch())
    comm = Comm(p, q, own, g, lx, ly, *rest[:n])
    comm.local(tiles)
    comm.barrier()
    comm.to_home()

    @pl.when(comm.home)
    def _():
        comm.begin()
        lead_factor(p, g, lx, *rest[n:], comm.ready, comm.ready_rest, comm.pump)
        comm.z_pass(7)
        comm.source_rest(7)
        comm.u_pass(6)
        comm.v_pass(5)

        def old(k, _):
            trail(p, q, k, lx, ly, tiles)
            return 0
        lax.fori_loop(0, 6, old, 0)
        comm.u_pass(7)
        comm.v_pass(6)
        trail(p, q, 6, lx, ly, tiles)

    @pl.when(jnp.logical_not(comm.home))
    def _():
        def turn(n, _):
            @pl.when(n < 8)
            def _():
                comm.z_pass(n)
                comm.s_send(n)
                comm.s_take(n)
                comm.source_rest(n)

            @pl.when((n >= 1) & (n < 9))
            def _():
                comm.u_pass(n - 1)

            @pl.when((n >= 2) & (n < 9))
            def _():
                comm.v_pass(n - 2)
                trail(p, q, n - 2, lx, ly, tiles)
            return 0
        lax.fori_loop(0, 9, turn, 0)

    comm.v_pass(7)
    trail(p, q, 7, lx, ly, tiles)
    put_out(q, lx, tiles, out_ref)
    comm.end()


def on_device(matrix):
    out = pl.pallas_call(
        entry,
        out_shape=jax.ShapeDtypeStruct((8 * B, 128), F32),
        in_specs=[pl.BlockSpec(memory_space=pltpu.VMEM)],
        out_specs=pl.BlockSpec(memory_space=pltpu.VMEM),
        scratch_shapes=[pltpu.VMEM((STEPS, SLOTS, B, B), F32), pltpu.VMEM((STEPS, 2, B, B), F32),
                        pltpu.VMEM((STEPS, 2, B, B), F32), pltpu.VMEM((2, B, 2 * B), F32)] + comm_scratch() + scratch(),
        compiler_params=pltpu.CompilerParams(vmem_limit_bytes=63 * 1024 * 1024, collective_id=0, has_side_effects=True),
        name="steps",
    )(matrix.reshape(8 * B, 128))
    return out.reshape(matrix.shape)


def solution(mesh):
    spec = P(None, "row", None, None, "col", None)
    return jax.shard_map(on_device, mesh=mesh, in_specs=(spec,), out_specs=spec, check_vma=False)
```

time: 234 us -> 197 us (0.84)
  the two profiles are of different devices: /device:TPU:240 before, /device:TPU:160 now
where the time goes in v6:
time: 197 us
  Pallas kernels  194 us (98%)
  local copies, waits for them, and re-layouts  2.91 us (1%)
    pallas_call x1, Pallas kernels, on_device(): pl.pallas_call(entry, out_shape=jax.ShapeDtypeStruct((8 * B, 128), F32),...  194 us

profile of v6, /device:TPU:160, one launch (start us, length us, event | category | flops | bytes accessed | tf_op | source)
XLA Modules:
  0.0 197.3 jit_solution(3631901653461885602)
XLA Ops:
  0.0 194.4 %steps.1 = f32[2048,128]{1,0:T(8,128)} custom-call(f32[2048,128]{1,0:T(8,128)} %bitcast.3), custom_call_target="tpu_custom_call" | custom-call | tf_op jit(solution)/shard_map/steps/pallas_call | solution.py:607
  194.4 2.9 %copy.4 = f32[2,1,256,2,1,256]{5,4,3,2,1,0:T(1,128)} copy(f32[2,1,256,2,1,256]{5,4,3,2,1,0:T(1,128)} %bitcast.2) | data formatting | bytes 2097152

commit v7 on v6

--- a/solution.py
+++ b/solution.py
@@ -103,7 +103,8 @@
         w_lo[at, :] = r_lo
         zpad[64:, :] = zpad[64:, :] + nn(lhs, jnp.concatenate([r_hi, r_hi, r_lo, r_lo], 0))
         return 0
-    lax.fori_loop(0, 4, group, 0)
+    for g in range(4):
+        group(g, 0)
 
 def blocks(tile, tb):
     low = lax.broadcasted_iota(jnp.int32, (256, 128), 1) < 64
@@ -140,17 +141,23 @@
                 apply(k, r, m)
                 return 0
             return lax.fori_loop(jnp.where(k == 2, 0, k - 1), k, term, 0)
-        lax.fori_loop(jnp.where(k > 0, k // 2, 5), 5, last, 0)
+        lax.fori_loop(jnp.where(k > 0, k // 2, 5), jnp.where(k > 0, k // 2 + 1, 5), last, 0)
         blocks(g[k, k], tb)
 
         def beside(i):
+            below = 4 - k // 2
+            now = below * jnp.where(k == 0, 0, jnp.where(k == 2, 2, 1))
             j = k + 1
             rows = jnp.maximum(5 - j // 2, 1)
-            for n in range(3):
-                turn = 3 * i + n
-                m = turn // rows
+            for n in range(4):
+                turn = 4 * i + n
+                first = turn < now
+                later = jnp.maximum(turn - now, 0)
+                m = later // rows
                 on = (m < k) & (j < STEPS) & (j != 2)
-                apply(jnp.where(on, j, 7), jnp.where(on, j // 2 + turn % rows, 0), jnp.where(on, m, 0))
+                apply(jnp.where(first, k, jnp.where(on, j, 7)),
+                      jnp.where(first, k // 2 + 1 + turn % below, jnp.where(on, j // 2 + later % rows, 0)),
+                      jnp.where(first, jnp.where(k == 2, turn // below, k - 1), jnp.where(on, m, 0)))
 
         factor_tile(tb, ud, lb, zpad, wh, wl, lambda i: pump(k, i), beside)
         ready_rest(k)
@@ -184,7 +191,7 @@
         def rest(r, _):
             keep(r, solve(r))
             return 0
-        lax.fori_loop(k // 2, 4, rest, 0)
+        lax.fori_loop((k + 1) // 2, 4, rest, 0)
         return 0
     lax.fori_loop(0, STEPS, step, 0)
 

time: 197 us -> 190 us (0.964)
  Pallas kernels: 194 us -> 187 us
    pallas_call x1, Pallas kernels: 194 us -> 187 us  [on_device(): pl.pallas_call(entry, out_shape=jax.ShapeDtypeStruct((8 * B, 128), F32),...]
where the time goes in v7:
time: 190 us
  Pallas kernels  187 us (98%)
  local copies, waits for them, and re-layouts  2.91 us (2%)
    pallas_call x1, Pallas kernels, on_device(): pl.pallas_call(entry, out_shape=jax.ShapeDtypeStruct((8 * B, 128), F32),...  187 us

profile of v7, /device:TPU:160, one launch (start us, length us, event | category | flops | bytes accessed | tf_op | source)
XLA Modules:
  0.0 189.5 jit_solution(18241431824258598886)
XLA Ops:
  0.0 186.6 %steps.1 = f32[2048,128]{1,0:T(8,128)} custom-call(f32[2048,128]{1,0:T(8,128)} %bitcast.3), custom_call_target="tpu_custom_call" | custom-call | tf_op jit(solution)/shard_map/steps/pallas_call | solution.py:614
  186.6 2.9 %copy.4 = f32[2,1,256,2,1,256]{5,4,3,2,1,0:T(1,128)} copy(f32[2,1,256,2,1,256]{5,4,3,2,1,0:T(1,128)} %bitcast.2) | data formatting | bytes 2097152

commit v8 on v7

--- a/solution.py
+++ b/solution.py
@@ -540,15 +540,20 @@
 
         self.waiting = True
         self.to_home()
+        self.waiting = False
 
         def one(k, _):
-            self.z_pass(k)
-            self.s_send(k)
-            self.source_rest(k)
-            self.u_pass(k)
-            self.v_pass(k)
+            self.drain_step(k)
             return 0
-        lax.fori_loop(0, STEPS, one, 0)
+        lax.fori_loop(jnp.where(self.home, 0, 5), STEPS, one, 0)
+
+    def drain_step(self, k):
+        self.waiting = True
+        self.z_pass(k)
+        self.s_send(k)
+        self.source_rest(k)
+        self.u_pass(k)
+        self.v_pass(k)
         self.waiting = False
 
 def comm_scratch():
@@ -601,6 +606,10 @@
             def _():
                 comm.v_pass(n - 2)
                 trail(p, q, n - 2, lx, ly, tiles)
+
+            @pl.when((n >= 3) & (n < 8))
+            def _():
+                comm.drain_step(n - 3)
             return 0
         lax.fori_loop(0, 9, turn, 0)
 

time: 190 us -> 189 us (level)
  no operation moved by 1% of the time
where the time goes in v8:
time: 189 us
  Pallas kernels  186 us (98%)
  local copies, waits for them, and re-layouts  2.91 us (2%)
    pallas_call x1, Pallas kernels, on_device(): pl.pallas_call(entry, out_shape=jax.ShapeDtypeStruct((8 * B, 128), F32),...  186 us

profile of v8, /device:TPU:160, one launch (start us, length us, event | category | flops | bytes accessed | tf_op | source)
XLA Modules:
  0.0 189.1 jit_solution(11915482081989637635)
XLA Ops:
  0.0 186.2 %steps.1 = f32[2048,128]{1,0:T(8,128)} custom-call(f32[2048,128]{1,0:T(8,128)} %bitcast.3), custom_call_target="tpu_custom_call" | custom-call | tf_op jit(solution)/shard_map/steps/pallas_call | solution.py:623
  186.2 2.9 %copy.4 = f32[2,1,256,2,1,256]{5,4,3,2,1,0:T(1,128)} copy(f32[2,1,256,2,1,256]{5,4,3,2,1,0:T(1,128)} %bitcast.2) | data formatting | bytes 2097152
